TPU v7x, 8 devices: a whole 2x2x1 slice. The times are simulated.
8 devices in a mesh: member: 1 (over z), lon: 2 (over y), lat: 4 (over x, core).
Axes of the slice: x: 2, y: 2, z: 1, core: 2. Of those that a mesh axis runs over, the one named last changes fastest.
Arguments:
- grid_field: float32 [4, 256, 256, 512], P('member', None, 'lat', 'lon')
- mix_weight: bfloat16 [256, 256, 256, 2], replicated
Outputs:
- output: float32 [4, 256, 256, 512], P('member', None, 'lat', 'lon')
All inputs are finite; a program needn't handle non-finite values.
Results may differ from a plain program's by a relative error of at most 0.00431334.
Values are sent between devices in bfloat16 or wider.
A program may use at most 1 GiB of HBM per device.

v0:
```python
import functools
import math
import numpy as np
import jax
import jax.numpy as jnp
from jax import lax
from jax.experimental import pallas as pl
from jax.experimental.pallas import tpu as pltpu
from jax.sharding import PartitionSpec as P


BF = jnp.bfloat16
F32 = jnp.float32
LB = 16
HALVES = ((16, 48), (32, 16, 16))
MB = 16
MG = 64
NV = 4
NT = (((1,), (1,)), ((), ()))
TN = (((0,), (0,)), ((), ()))


def legendre_tables(n_lat, n_lon, n_deg):
    t = (np.arange(n_lat) + 0.5) * (math.pi / n_lat)
    x = np.cos(t)
    m = np.arange(n_deg)
    steps = np.concatenate([[0.0], np.cumsum(0.5 * np.log((2.0 * m[1:] + 1.0) / (2.0 * m[1:])))])
    diag = np.exp(0.5 * math.log(0.5) + steps[:, None] + m[:, None] * np.log(np.sin(t))[None, :])
    tab = np.zeros((n_deg, n_deg, n_lat))
    mm = m[:, None].astype(np.float64)
    prev1 = np.zeros((n_deg, n_lat))
    prev2 = np.zeros((n_deg, n_lat))
    for l in range(n_deg):
        a = np.sqrt((4.0 * l * l - 1.0) / np.maximum(l * l - mm * mm, 1.0)) if l > 0 else np.ones_like(mm)
        b = np.sqrt(np.maximum((l - 1.0) ** 2 - mm * mm, 0.0) / max(4.0 * (l - 1.0) ** 2 - 1.0, 1.0))
        cur = np.where(mm < l, a * (x[None, :] * prev1 - b * prev2), 0.0)
        cur[l] = diag[l]
        tab[:, l, :] = cur
        prev2 = prev1
        prev1 = cur
    n = np.arange(1, n_lat // 2 + 1)
    series = np.sum(np.cos(2.0 * t[:, None] * n[None, :]) / (4.0 * n * n - 1.0), axis=1)
    w = (2.0 / n_lat) * (1.0 - 2.0 * series)

    def pack(p):
        p = p.astype(np.float32).astype(BF).reshape(n_deg, n_deg // (2 * LB), 2, LB, n_lat)
        return np.ascontiguousarray(p.transpose(0, 2, 1, 3, 4)).reshape(n_deg, 2, n_deg // 2, n_lat)

    return pack(tab * (w / n_lon)), pack(tab)


def dft_tables(n_lon, n_deg):
    ang = ((np.arange(n_deg)[:, None] * np.arange(n_lon)[None, :]) % n_lon) * (2.0 * math.pi / n_lon)
    c_m = np.where(np.arange(n_deg) == 0, 1.0, 2.0)[:, None, None]
    fwd = np.stack([np.cos(ang), -np.sin(ang)], axis=1)

    def pack(p):
        p = p.astype(np.float32).astype(BF).reshape(2 * n_deg, 2, n_lon // 2)
        return np.ascontiguousarray(np.stack([p, p[:, ::-1]])).reshape(2, 2 * n_deg, n_lon)

    return pack(fwd), pack(c_m * fwd)


def cast_kernel(s_ref, *refs):
    n = len(refs) // 2
    for t in range(n):
        refs[n + t][...] = refs[t][0].astype(BF)


def fwd_dft_kernel(s_ref, tab_ref, *refs):
    pieces, (out, scr, rc) = refs[:8], refs[-3:]
    r = s_ref[2]
    rows = pieces[0].shape[1]
    cols = pieces[0].shape[2]
    nms = out.shape[0]

    def body(c2, carry):
        for u in range(2):
            c = c2 * 2 + u
            for t in range(8):
                row = pl.multiple_of(((t & 3) ^ r) * rows, rows)
                q = t >> 2
                rc[u, pl.ds(row, rows), q * cols:(q + 1) * cols] = pieces[t][c]
        for u in range(2):
            c = c2 * 2 + u
            res = lax.dot_general(tab_ref[0], rc[u], NT, preferred_element_type=F32)
            for j in range(res.shape[1] // 128):
                scr[j, pl.ds(c, nms, stride=16), :] = res[:, j * 128:(j + 1) * 128]
        return carry

    lax.fori_loop(0, 8, body, 0)

    def flush(i, carry):
        for j in range(scr.shape[0]):
            blk = scr[j, pl.ds(pl.multiple_of(i * 512, 512), 512), :]
            out[pl.ds(i * 32, 32), :, j * 128:(j + 1) * 128] = blk.reshape(32, 16, 128).astype(BF)
        return carry

    lax.fori_loop(0, nms // 32, flush, 0)


def fwd_leg_kernel(nf, s_ref, *refs):
    pws, fs = refs[:NV], refs[NV:NV + nf]
    mine, send = refs[-2 * NV:-NV], refs[-NV:]
    h = s_ref[3]
    gran = pl.program_id(0) // (MG // MB)
    nl = pws[0].shape[2]
    for g in range(NV):
        @pl.when(gran == g)
        def _(g=g):
            def body(m8, carry):
                for u in range(8):
                    m = m8 * 8 + u
                    x = jnp.concatenate([f[2 * m + s] for s in range(2) for f in fs], axis=0)
                    p = jnp.concatenate([pws[v][m, h] for v in range(g, NV)] + [pws[v][m, 1 - h] for v in range(g, NV)], axis=0)
                    res = lax.dot_general(p, x, NT, preferred_element_type=F32).astype(BF)
                    for v in range(g, NV):
                        mine[v][m] = res[(v - g) * nl:(v - g + 1) * nl]
                        send[v][m] = res[(NV + v - 2 * g) * nl:(NV + v - 2 * g + 1) * nl]
                return carry

            lax.fori_loop(0, MB // 8, body, 0)


def mix_kernel(vs, s_ref, wre, wim, *refs):
    ins = {v: refs[4 * n:4 * n + 4] for n, v in enumerate(vs)}
    outs = {v: refs[8 + 4 * n:12 + 4 * n] for n, v in enumerate(vs)}
    scr_a, scr_b = refs[-2:]
    h = s_ref[3]
    for n, v in enumerate(vs):
        @pl.when(pl.program_id(0) // 2 == n)
        def _(v=v):
            nm = MG * (v + 1)

            def fill(i, carry):
                rows = pl.ds(pl.multiple_of(i * 512, 512), 512)
                for half in range(2):
                    scr_a[2 * h + half, rows, :] = ins[v][half][pl.ds(i * 32, 32)].astype(F32).reshape(512, 128)
                    scr_a[2 - 2 * h + half, rows, :] = ins[v][2 + half][pl.ds(i * 32, 32)].astype(F32).reshape(512, 128)
                return carry

            lax.fori_loop(0, nm // 32, fill, 0)

            def body(li2, carry):
                for u in range(2):
                    li = li2 * 2 + u
                    lhs = jnp.concatenate([scr_a[b, pl.ds(li, nm, stride=LB), :].astype(BF) for b in range(4)], axis=1)
                    wr, wi = wre[li], wim[li]
                    ni = -wi
                    cg = wr.shape[0] // 4
                    rhs_re = jnp.concatenate([w[b * cg:(b + 1) * cg] for b in range(4) for w in (wr, ni)], axis=0)
                    rhs_im = jnp.concatenate([w[b * cg:(b + 1) * cg] for b in range(4) for w in (wi, wr)], axis=0)
                    bre = jnp.dot(lhs, rhs_re, preferred_element_type=F32)
                    bim = jnp.dot(lhs, rhs_im, preferred_element_type=F32)
                    for b in range(2):
                        scr_b[b, pl.ds(li, nm, stride=LB), :] = bre[:, b * 128:(b + 1) * 128]
                        scr_b[2 + b, pl.ds(li, nm, stride=LB), :] = bim[:, b * 128:(b + 1) * 128]
                return carry

            lax.fori_loop(0, LB // 2, body, 0)
            low = lax.broadcasted_iota(jnp.int32, (512, 128), 1) < 64

            def flush(i, carry):
                rows = pl.ds(pl.multiple_of(i * 512, 512), 512)
                for side, hh in ((0, h), (2, 1 - h)):
                    re, im = scr_b[hh, rows, :], scr_b[2 + hh, rows, :]
                    first = jnp.where(low, re, pltpu.roll(im, 64, 1))
                    second = jnp.where(low, pltpu.roll(re, 64, 1), im)
                    outs[v][side][pl.ds(i * 32, 32)] = first.reshape(32, LB, 128).astype(BF)
                    outs[v][side + 1][pl.ds(i * 32, 32)] = second.reshape(32, LB, 128).astype(BF)
                return carry

            lax.fori_loop(0, nm // 32, flush, 0)


def inv_leg_kernel(no, s_ref, *refs):
    pis, bm, br = refs[:NV], refs[NV:2 * NV], refs[2 * NV:3 * NV]
    outs = refs[-no:]
    h = s_ref[3]
    gran = pl.program_id(0) // (MG // MB)
    for g in range(NV):
        @pl.when(gran == g)
        def _(g=g):
            def body(m8, carry):
                for u in range(8):
                    m = m8 * 8 + u
                    b = jnp.concatenate([bm[v][m] for v in range(g, NV)] + [br[v][m] for v in range(g, NV)], axis=0)
                    p = jnp.concatenate([pis[v][m, h] for v in range(g, NV)] + [pis[v][m, 1 - h] for v in range(g, NV)], axis=0)
                    y = lax.dot_general(b, p, TN, preferred_element_type=F32).astype(BF)
                    off = 0
                    for o in outs:
                        n = o.shape[1]
                        for s in range(2):
                            o[2 * m + s] = y[s * 64 + off:s * 64 + off + n]
                        off += n
                return carry

            lax.fori_loop(0, MB // 8, body, 0)


def inv_dft_kernel(s_ref, tab_ref, g_ref, *refs):
    pieces, (scr, yc) = refs[-10:-2], refs[-2:]
    r = s_ref[2]
    rows = pieces[0].shape[1]
    cols = pieces[0].shape[2]
    nms = g_ref.shape[0]

    def fill(i, carry):
        for j in range(scr.shape[0]):
            blk = g_ref[pl.ds(i * 32, 32), :, j * 128:(j + 1) * 128].astype(F32)
            scr[j, pl.ds(pl.multiple_of(i * 512, 512), 512), :] = blk.reshape(512, 128)
        return carry

    lax.fori_loop(0, nms // 32, fill, 0)

    def body(c2, carry):
        for u in range(2):
            c = c2 * 2 + u
            g = jnp.concatenate([scr[j, pl.ds(c, nms, stride=16), :].astype(BF) for j in range(scr.shape[0])], axis=1)
            yc[u] = lax.dot_general(g, tab_ref[0], TN, preferred_element_type=F32).astype(BF)
        for u in range(2):
            c = c2 * 2 + u
            for t in range(8):
                row = pl.multiple_of(((t & 3) ^ r) * rows, rows)
                q = t >> 2
                pieces[t][c] = yc[u, pl.ds(row, rows), q * cols:(q + 1) * cols]
        return carry

    lax.fori_loop(0, 8, body, 0)


def gelu(y):
    return 0.5 * y * (1.0 + lax.erf(y * math.sqrt(0.5)))


def final_kernel(s_ref, f_ref, *refs):
    pieces, (out, buf) = refs[:8], refs[-2:]
    t = pl.program_id(0)
    for n in range(8):
        @pl.when(t == n)
        def _(n=n):
            buf[...] = pieces[n][...]

    def body(c, carry):
        out[0, c] = f_ref[0, c] + gelu(buf[c].astype(F32))
        return carry

    lax.fori_loop(0, buf.shape[0], body, 0)


def call(kernel, grid, in_specs, out_specs, out_shape, flops, nbytes, scratch=(), deps=(), alias=None):
    fn = pl.pallas_call(
        kernel,
        grid_spec=pltpu.PrefetchScalarGridSpec(
            num_scalar_prefetch=1, grid=grid,
            in_specs=list(in_specs) + [pl.BlockSpec(memory_space=pl.ANY)] * len(deps),
            out_specs=out_specs, scratch_shapes=list(scratch)),
        out_shape=out_shape,
        input_output_aliases=alias or {},
        compiler_params=pltpu.CompilerParams(dimension_semantics=("arbitrary",) * len(grid), vmem_limit_bytes=58 * 2 ** 20),
        cost_estimate=pl.CostEstimate(flops=int(flops), bytes_accessed=int(nbytes), transcendentals=0),
    )
    return lambda *args: fn(*args, *deps)


def solution(mesh):
    lat_devs = mesh.shape['lat']
    lon_devs = mesh.shape['lon']
    nd = lat_devs * lon_devs

    def local_layer(grid_field, mix_weight):
        batch, channels, row_count, col_count = grid_field.shape
        n_lat = row_count * lat_devs
        n_lon = col_count * lon_devs
        n_deg = mix_weight.shape[0]
        half_c = batch * channels // nd
        nms = 2 * n_deg
        lv = n_deg // 2 // NV
        q = lax.axis_index('lon')
        r = lax.axis_index('lat')
        me = q * lat_devs + r
        h = r % 2
        scal = jnp.stack([me, q, r, h]).astype(jnp.int32)
        pw_np, pi_np = legendre_tables(n_lat, n_lon, n_deg)
        tf_np, ti_np = dft_tables(n_lon, n_deg)
        pw, pi, tf, ti = jnp.asarray(pw_np), jnp.asarray(pi_np), jnp.asarray(tf_np), jnp.asarray(ti_np)
        f8 = grid_field.reshape(nd, half_c, row_count, col_count)

        def swap(x, t):
            if t == 0:
                return x
            return lax.ppermute(x, ('lon', 'lat'), [(s, s ^ t) for s in range(nd)])

        def piece(cc):
            return jax.ShapeDtypeStruct((cc, row_count, col_count), BF)

        tab_spec = pl.BlockSpec((1, nms, n_lon), lambda i, s: (s[1], 0, 0))
        piece_spec16 = pl.BlockSpec((16, row_count, col_count), lambda i, s: (i, 0, 0))
        dft_scratch = [pltpu.VMEM((n_lat // 128, nms * 16, 128), F32), pltpu.VMEM((2, n_lat, n_lon), BF)]

        def cast_chunk(c0, cc):
            cb = 8
            base = c0 // cb
            return call(
                cast_kernel, (cc // cb,),
                [pl.BlockSpec((1, cb, row_count, col_count), functools.partial(lambda t, i, s: (s[0] ^ t, base + i, 0, 0), t)) for t in range(nd)],
                [pl.BlockSpec((cb, row_count, col_count), lambda i, s: (i, 0, 0))] * nd,
                [piece(cc)] * nd, 1e6, nd * cc * row_count * col_count * 6)(scal, *([f8] * nd))

        def dft_chunk(pieces, cc, deps):
            return call(
                fwd_dft_kernel, (cc // 16,),
                [tab_spec] + [piece_spec16] * nd,
                pl.BlockSpec((nms, 16, n_lat), lambda i, s: (0, i, 0)),
                jax.ShapeDtypeStruct((nms, cc, n_lat), BF),
                4.0 * cc * nms * n_lat * n_lon, cc * nms * n_lat * 6, dft_scratch, deps)(scal, tf, *pieces)

        last = [MG // MB * (v + 1) - 1 for v in range(NV)]
        tri_specs = [pl.BlockSpec((MB, 2, lv, n_lat), functools.partial(lambda v, i, s: (jnp.minimum(i, last[v]), 0, v, 0), v)) for v in range(NV)]
        spec_specs = [pl.BlockSpec((MB, lv, half_c), functools.partial(lambda v, i, s: (jnp.minimum(i, last[v]), 0, 0), v)) for v in range(NV)]
        spec_shapes = [jax.ShapeDtypeStruct((MG * (v + 1), lv, half_c), BF) for v in range(NV)]

        def f_spec(cc):
            return pl.BlockSpec((2 * MB, cc, n_lat), lambda i, s: (i, 0, 0))

        def leg_fwd(fs):
            res = call(
                functools.partial(fwd_leg_kernel, len(fs)), (n_deg // MB,),
                tri_specs + [f_spec(f.shape[1]) for f in fs],
                spec_specs * 2, spec_shapes * 2,
                1.3 * n_deg * n_deg * n_lat * half_c, 50e6)(scal, *([pw] * NV), *fs)
            return res[:NV], res[NV:]

        def leg_inv(half, mine, recv, deps=()):
            return call(
                functools.partial(inv_leg_kernel, len(HALVES[half])), (n_deg // MB,),
                tri_specs + spec_specs * 2,
                [f_spec(cc) for cc in HALVES[half]],
                [jax.ShapeDtypeStruct((nms, cc, n_lat), BF) for cc in HALVES[half]],
                1.3 * n_deg * n_deg * n_lat * half_c, 50e6, (), deps)(scal, *([pi] * NV), *mine, *recv)

        sizes = HALVES[0] + HALVES[1]
        starts = [sum(sizes[:k]) for k in range(len(sizes))]
        recv = []
        for c0, cc in zip(starts, sizes):
            k = len(recv)
            pieces = cast_chunk(c0, cc)
            recv.append([swap(p, t) for t, p in enumerate(pieces)])

        w = mix_weight.reshape(n_deg // (2 * LB), 2, LB, channels, channels, 2)
        w = lax.dynamic_index_in_dim(w, h, axis=1, keepdims=False).reshape(n_deg // 2, channels, channels, 2)
        w_re, w_im = w[..., 0], w[..., 1]

        a_mine, a_recv, prev = [], [], []
        k = 0
        for half in range(2):
            fs = []
            for cc in HALVES[half]:
                deps = list(prev)
                if k == 1:
                    deps += [w_re, w_im]
                elif k == len(HALVES[0]):
                    deps += [a_mine[0][0]]
                fs.append(dft_chunk(recv[k], cc, deps))
                prev = fs[-1:]
                k += 1
            mine, send = leg_fwd(fs)
            a_mine.append(mine)
            got = [None] * NV
            for v in reversed(range(NV)):
                got[v] = swap(send[v], 1)
            a_recv.append(got)

        def mix(vs):
            first = vs[0] * 2
            jump = [lambda j: jnp.minimum(j, 1), lambda j: jnp.maximum(j - 2, 0)]
            w_spec = pl.BlockSpec((LB, channels, channels), lambda j, s: (jnp.where(j < 2, first + j, first + j - 4), 0, 0))
            specs, shapes, args = [], [], []
            for n, v in enumerate(vs):
                specs += [pl.BlockSpec((MG * (v + 1), LB, half_c), functools.partial(lambda n, j, s: (0, jump[n](j), 0), n))] * 4
                shapes += [spec_shapes[v]] * 4
                args += [a_mine[0][v], a_mine[1][v], a_recv[0][v], a_recv[1][v]]
            rows = MG * (vs[0] + 1) * LB
            return call(
                functools.partial(mix_kernel, vs), (4,), [w_spec, w_spec] + specs, specs, shapes,
                8.0 * 4 * LB * MG * (vs[0] + 1) * channels * channels, 60e6,
                [pltpu.VMEM((4, rows, 128), F32), pltpu.VMEM((4, rows, 128), F32)])(scal, w_re, w_im, *args)

        b_mine = [[None] * NV, [None] * NV]
        b_recv = [[None] * NV, [None] * NV]
        for vs in ((3, 2), (1, 0)):
            res = mix(vs)
            for n, v in enumerate(vs):
                for half in range(2):
                    b_mine[half][v] = res[4 * n + half]
                    b_recv[half][v] = swap(res[4 * n + 2 + half], 1)

        def idft_chunk(g):
            cc = g.shape[1]
            return call(
                inv_dft_kernel, (cc // 16,),
                [tab_spec, pl.BlockSpec((nms, 16, n_lat), lambda i, s: (0, i, 0))],
                [piece_spec16] * nd, [piece(cc)] * nd,
                4.0 * cc * nms * n_lat * n_lon, cc * nms * n_lat * 6, dft_scratch)(scal, ti, g)

        def final_chunk(c0, cc, pieces, out):
            cb = 8
            base, nb = c0 // cb, cc // cb
            big = pl.BlockSpec((1, cb, row_count, col_count), lambda t, i, s: (s[0] ^ t, base + i, 0, 0))

            def own(n):
                return pl.BlockSpec((cb, row_count, col_count),
                                    lambda t, i, s: (jnp.where(t == n, i, jnp.where(t < n, 0, nb - 1)), 0, 0))

            deps = [] if out is None else [out]
            return call(
                final_kernel, (nd, nb), [big] + [own(n) for n in range(nd)], big,
                jax.ShapeDtypeStruct(f8.shape, F32), 40 * nd * cc * row_count * col_count, 10 * nd * cc * row_count * col_count,
                [pltpu.VMEM((cb, row_count, col_count), BF)], deps,
                {2 + nd: 0} if deps else None)(scal, f8, *pieces)

        k = 0
        out = None
        dep = ()
        for half in range(2):
            gs = leg_inv(half, b_mine[half], b_recv[half], dep)
            for g in gs:
                cc = g.shape[1]
                pieces = idft_chunk(g)
                if k == 0:
                    dep = (pieces[0],)
                got = [swap(p, t) for t, p in enumerate(pieces)]
                if k < len(sizes) - 1:
                    out = final_chunk(starts[k], cc, got, out)
                else:
                    for t, p in enumerate(got):
                        src = lax.dynamic_slice(f8, (me ^ t, starts[k], 0, 0), (1, cc, row_count, col_count))
                        new = src + gelu(p.astype(F32))[None]
                        out = lax.dynamic_update_slice(out, new, (me ^ t, starts[k], 0, 0))
                k += 1
        return out.reshape(grid_field.shape)

    field_spec = P('member', None, 'lat', 'lon')
    return jax.shard_map(local_layer, mesh=mesh, in_specs=(field_spec, P()), out_specs=field_spec, check_vma=False)
```

profile of v0, /device:TPU:0, one launch (start us, length us, event | category | flops | bytes accessed | tf_op | source)
XLA Modules:
  0.0 1094.5 jit_solution(15124997603098149456)
XLA Ops:
  36.4 21.1 %collective-permute-done.4.refs_5_ = bf16[16,64,256]{2,1,0:T(8,128)(2,1)} collective-permute-done((bf16[16,64,256]{2,1,0:T(8,128)(2,1)}, bf16[16,64,256]{2,1,0:T(8,128)(2,1)}, u32[]{:S(2)}, u32[]{:S(2)}) %collective-permute-start.4) | collective-permute-done | bytes 524320 | tf_op jit(solution)/shard_map/ppermute | solution.py:292
  79.3 13.7 %shard_map.66 = (bf16[48,64,256]{2,1,0:T(8,128)(2,1)}, bf16[48,64,256]{2,1,0:T(8,128)(2,1)}, bf16[48,64,256]{2,1,0:T(8,128)(2,1)}, bf16[48,64,256]{2,1,0:T(8,128...) custom-call(s32[4]{0:T(128)} %pad_add_fusion.s_ref, ...), custom_call_target="tpu_custom_call" | custom-call | flops 1000000 | bytes 37748736 | tf_op jit(solution)/shard_map/pallas_call | solution.py:263
  117.3 26.7 %constant_dynamic-slice_fusion = bf16[8,1,16,256,256,2]{4,5,3,2,1,0:T(2,128)(2,1)} fusion(bf16[8,2,16,256,256,2]{4,5,3,2,1,0:T(2,128)(2,1)} %bitcast.5, s32[]{:T(128)S(6)} %select_n.44), kind=kLoop, calls=%fused_computation.66 | loop fusion | bytes 67108864 | tf_op jit(solution)/shard_map/jit(dynamic_index_in_dim)/dynamic_slice | solution.py:351
  144.0 22.7 %copy.11 = bf16[8,1,16,256,256,2]{4,3,2,0,5,1:T(8,128)(2,1)} copy(bf16[8,1,16,256,256,2]{4,5,3,2,1,0:T(2,128)(2,1)} %constant_dynamic-slice_fusion) | data formatting | bytes 67108864
  170.3 76.6 %collective-permute-done.11.refs_5_ = bf16[48,64,256]{2,1,0:T(8,128)(2,1)S(1)} collective-permute-done((bf16[48,64,256]{2,1,0:T(8,128)(2,1)}, bf16[48,64,256]{2,1,0:T(8,128)(2,1)S(1)}, u32[]{:S(2)}, u32[]{:S(2)}) %collective-permute-start.11) | collective-permute-done | bytes 1572896 | tf_op jit(solution)/shard_map/ppermute | solution.py:292
  248.3 23.0 %slice_bitcast_fusion = (bf16[128,256,256]{2,1,0:T(8,128)(2,1)}, bf16[128,256,256]{2,1,0:T(8,128)(2,1)}) fusion(bf16[128,256,256,2]{2,1,0,3:T(8,128)(2,1)} %bitcast.60), kind=kLoop, calls=%fused_computation | loop fusion | bytes 67108864 | tf_op jit(solution)/shard_map/squeeze | solution.py:352
  287.9 15.5 %collective-permute-done.9.refs_3_ = bf16[48,64,256]{2,1,0:T(8,128)(2,1)} collective-permute-done((bf16[48,64,256]{2,1,0:T(8,128)(2,1)}, bf16[48,64,256]{2,1,0:T(8,128)(2,1)}, u32[]{:S(2)}, u32[]{:S(2)}) %collective-permute-start.9) | collective-permute-done | bytes 1572896 | tf_op jit(solution)/shard_map/ppermute | solution.py:292
  306.6 25.3 %shard_map.67.refs_5_.refs_8_ = bf16[512,48,256]{2,1,0:T(8,128)(2,1)} custom-call(s32[4]{0:T(128)} %pad_add_fusion.s_ref, bf16[2,512,512]{2,1,0:T(8,128)(2,1)} %constant.58.clone.tab_ref, bf16[48,64,256]{2,1,0:T(8,128)(2,1)} %get-tuple-element.130.refs_0_, bf16[48,64,256]{2,1,0:T(8,128)(2,1)} %collective-permute-done.7.refs_1_, ...), custom_call_target="tpu_custom_call" | custom-call | flops 12884901888 | bytes 37748736 | tf_op jit(solution)/shard_map/pallas_call | solution.py:263
  331.9 24.4 %shard_map.68 = (bf16[64,32,128]{2,1,0:T(8,128)(2,1)}, bf16[128,32,128]{2,1,0:T(8,128)(2,1)}, bf16[192,32,128]{2,1,0:T(8,128)(2,1)}, bf16[256,32,128]{2,1,0:T(8,...) custom-call(s32[4]{0:T(128)} %pad_add_fusion.s_ref, ...), custom_call_target="tpu_custom_call" | custom-call | flops 2791728640 | bytes 50000000 | tf_op jit(solution)/shard_map/pallas_call | solution.py:263
  356.9 20.1 %collective-permute-done.18.refs_5_ = bf16[32,64,256]{2,1,0:T(8,128)(2,1)} collective-permute-done((bf16[32,64,256]{2,1,0:T(8,128)(2,1)S(1)}, bf16[32,64,256]{2,1,0:T(8,128)(2,1)}, u32[]{:S(2)}, u32[]{:S(2)}) %collective-permute-start.18) | collective-permute-done | bytes 1048608 | tf_op jit(solution)/shard_map/ppermute | solution.py:292
  381.3 18.7 %shard_map.70.refs_8_.refs_4_ = bf16[512,32,256]{2,1,0:T(8,128)(2,1)} custom-call(s32[4]{0:T(128)} %pad_add_fusion.s_ref, bf16[2,512,512]{2,1,0:T(8,128)(2,1)} %constant.58.clone.tab_ref, bf16[32,64,256]{2,1,0:T(8,128)(2,1)} %get-tuple-element.139.refs_0_, bf16[32,64,256]{2,1,0:T(8,128)(2,1)} %collective-permute-done.14.refs_1_, ...), custom_call_target="tpu_custom_call" | custom-call | flops 8589934592 | bytes 25165824 | tf_op jit(solution)/shard_map/pallas_call | solution.py:263
  434.6 24.2 %shard_map.75 = (bf16[64,32,128]{2,1,0:T(8,128)(2,1)}, bf16[128,32,128]{2,1,0:T(8,128)(2,1)}, bf16[192,32,128]{2,1,0:T(8,128)(2,1)}, bf16[256,32,128]{2,1,0:T(8,...) custom-call(s32[4]{0:T(128)} %pad_add_fusion.s_ref, ...), custom_call_target="tpu_custom_call" | custom-call | flops 2791728640 | bytes 50000000 | tf_op jit(solution)/shard_map/pallas_call | solution.py:263
  473.1 45.3 %shard_map.77 = (bf16[256,32,128]{2,1,0:T(8,128)(2,1)}, bf16[256,32,128]{2,1,0:T(8,128)(2,1)}, bf16[256,32,128]{2,1,0:T(8,128)(2,1)}, bf16[256,32,128]{2,1,0:T(8...) custom-call(s32[4]{0:T(128)} %pad_add_fusion.s_ref, ...), custom_call_target="tpu_custom_call" | custom-call | flops 8589934592 | bytes 60000000 | tf_op jit(solution)/shard_map/pallas_call | solution.py:263
  519.0 24.7 %shard_map.76 = (bf16[128,32,128]{2,1,0:T(8,128)(2,1)}, bf16[128,32,128]{2,1,0:T(8,128)(2,1)}, bf16[128,32,128]{2,1,0:T(8,128)(2,1)}, bf16[128,32,128]{2,1,0:T(8...) custom-call(s32[4]{0:T(128)} %pad_add_fusion.s_ref, ...), custom_call_target="tpu_custom_call" | custom-call | flops 4294967296 | bytes 60000000 | tf_op jit(solution)/shard_map/pallas_call | solution.py:263
  549.8 23.8 %shard_map.78 = (bf16[512,16,256]{2,1,0:T(8,128)(2,1)}, bf16[512,48,256]{2,1,0:T(8,128)(2,1)}) custom-call(s32[4]{0:T(128)} %pad_add_fusion.s_ref, bf16[256,2,128,256]{3,2,1,0:T(8,128)(2,1)} %constant.57.clone.refs_0_.refs_1_.refs_2_.refs_3_, bf16[256,2,128,256]{3,2,1,0:T(8,128)(2,1)} %constant.57.clone.refs_0_.refs_1_.refs_2_.refs_3_, ...), custom_call_target="tpu_custom_call" | custom-call | flops 2791728640 | bytes 50000000 | tf_op jit(solution)/shard_map/pallas_call | solution.py:263
  573.6 12.3 %shard_map.79 = (bf16[16,64,256]{2,1,0:T(8,128)(2,1)}, bf16[16,64,256]{2,1,0:T(8,128)(2,1)}, bf16[16,64,256]{2,1,0:T(8,128)(2,1)}, bf16[16,64,256]{2,1,0:T(8,128...) custom-call(s32[4]{0:T(128)} %pad_add_fusion.s_ref, ...), custom_call_target="tpu_custom_call" | custom-call | flops 4294967296 | bytes 12582912 | tf_op jit(solution)/shard_map/pallas_call | solution.py:263
  591.1 23.8 %shard_map.80 = (bf16[512,32,256]{2,1,0:T(8,128)(2,1)}, bf16[512,16,256]{2,1,0:T(8,128)(2,1)}, bf16[512,16,256]{2,1,0:T(8,128)(2,1)}) custom-call(s32[4]{0:T(128)} %pad_add_fusion.s_ref, bf16[256,2,128,256]{3,2,1,0:T(8,128)(2,1)} %constant.57.clone.refs_0_.refs_1_.refs_2_.refs_3_, bf16[256,2,128,256]{3,2,1,0:T(8,128)(2,1)} %constant.57.clone.refs_0_.refs_1_.refs_2_.refs_3_, ...), custom_call_target="tpu_custom_call" | custom-call | flops 2791728640 | bytes 50000000 | tf_op jit(solution)/shard_map/pallas_call | solution.py:263
  614.9 12.4 %shard_map.81 = (bf16[16,64,256]{2,1,0:T(8,128)(2,1)}, bf16[16,64,256]{2,1,0:T(8,128)(2,1)}, bf16[16,64,256]{2,1,0:T(8,128)(2,1)}, bf16[16,64,256]{2,1,0:T(8,128...) custom-call(s32[4]{0:T(128)} %pad_add_fusion.s_ref, ...), custom_call_target="tpu_custom_call" | custom-call | flops 4294967296 | bytes 12582912 | tf_op jit(solution)/shard_map/pallas_call | solution.py:263
  630.9 19.8 %shard_map.82 = (bf16[32,64,256]{2,1,0:T(8,128)(2,1)}, bf16[32,64,256]{2,1,0:T(8,128)(2,1)}, bf16[32,64,256]{2,1,0:T(8,128)(2,1)}, bf16[32,64,256]{2,1,0:T(8,128...) custom-call(s32[4]{0:T(128)} %pad_add_fusion.s_ref, ...), custom_call_target="tpu_custom_call" | custom-call | flops 8589934592 | bytes 25165824 | tf_op jit(solution)/shard_map/pallas_call | solution.py:263
  664.7 27.3 %shard_map.83 = (bf16[48,64,256]{2,1,0:T(8,128)(2,1)}, bf16[48,64,256]{2,1,0:T(8,128)(2,1)}, bf16[48,64,256]{2,1,0:T(8,128)(2,1)}, bf16[48,64,256]{2,1,0:T(8,128...) custom-call(s32[4]{0:T(128)} %pad_add_fusion.s_ref, ...), custom_call_target="tpu_custom_call" | custom-call | flops 12884901888 | bytes 37748736 | tf_op jit(solution)/shard_map/pallas_call | solution.py:263
  692.0 27.7 %collective-permute-done.53.refs_3_ = bf16[16,64,256]{2,1,0:T(8,128)(2,1)S(1)} collective-permute-done((bf16[16,64,256]{2,1,0:T(8,128)(2,1)}, bf16[16,64,256]{2,1,0:T(8,128)(2,1)S(1)}, u32[]{:S(2)}, u32[]{:S(2)}) %collective-permute-start.53) | collective-permute-done | bytes 524320 | tf_op jit(solution)/shard_map/ppermute | solution.py:292
  724.1 21.9 %collective-permute-done.62.refs_5_ = bf16[32,64,256]{2,1,0:T(8,128)(2,1)S(1)} collective-permute-done((bf16[32,64,256]{2,1,0:T(8,128)(2,1)}, bf16[32,64,256]{2,1,0:T(8,128)(2,1)S(1)}, u32[]{:S(2)}, u32[]{:S(2)}) %collective-permute-start.62) | collective-permute-done | bytes 1048608 | tf_op jit(solution)/shard_map/ppermute | solution.py:292
  747.6 33.2 %collective-permute-done.63.refs_6_ = bf16[32,64,256]{2,1,0:T(8,128)(2,1)S(1)} collective-permute-done((bf16[32,64,256]{2,1,0:T(8,128)(2,1)}, bf16[32,64,256]{2,1,0:T(8,128)(2,1)S(1)}, u32[]{:S(2)}, u32[]{:S(2)}) %collective-permute-start.63) | collective-permute-done | bytes 1048608 | tf_op jit(solution)/shard_map/ppermute | solution.py:292
  781.6 20.0 %collective-permute-done.64.refs_7_ = bf16[32,64,256]{2,1,0:T(8,128)(2,1)S(1)} collective-permute-done((bf16[32,64,256]{2,1,0:T(8,128)(2,1)}, bf16[32,64,256]{2,1,0:T(8,128)(2,1)S(1)}, u32[]{:S(2)}, u32[]{:S(2)}) %collective-permute-start.64) | collective-permute-done | bytes 1048608 | tf_op jit(solution)/shard_map/ppermute | solution.py:292
  805.5 29.3 %collective-permute-done.67.refs_3_ = bf16[48,64,256]{2,1,0:T(8,128)(2,1)} collective-permute-done((bf16[48,64,256]{2,1,0:T(8,128)(2,1)}, bf16[48,64,256]{2,1,0:T(8,128)(2,1)}, u32[]{:S(2)}, u32[]{:S(2)}) %collective-permute-start.67) | collective-permute-done | bytes 1572896 | tf_op jit(solution)/shard_map/ppermute | solution.py:292
  837.9 99.3 %collective-permute-done.69.refs_5_ = bf16[48,64,256]{2,1,0:T(8,128)(2,1)} collective-permute-done((bf16[48,64,256]{2,1,0:T(8,128)(2,1)}, bf16[48,64,256]{2,1,0:T(8,128)(2,1)}, u32[]{:S(2)}, u32[]{:S(2)}) %collective-permute-start.69) | collective-permute-done | bytes 1572896 | tf_op jit(solution)/shard_map/ppermute | solution.py:292
  939.6 12.4 %shard_map.88 = (bf16[16,64,256]{2,1,0:T(8,128)(2,1)}, bf16[16,64,256]{2,1,0:T(8,128)(2,1)}, bf16[16,64,256]{2,1,0:T(8,128)(2,1)}, bf16[16,64,256]{2,1,0:T(8,128...) custom-call(s32[4]{0:T(128)} %pad_add_fusion.s_ref, ...), custom_call_target="tpu_custom_call" | custom-call | flops 4294967296 | bytes 12582912 | tf_op jit(solution)/shard_map/pallas_call | solution.py:263
  953.8 15.1 %shard_map.84.refs_8_ = f32[8,128,64,256]{3,2,1,0:T(8,128)} custom-call(s32[4]{0:T(128)} %pad_add_fusion.s_ref, f32[8,128,64,256]{3,2,1,0:T(8,128)} %bitcast.4.refs_0_.refs_1_.refs_2_.refs_3_.refs_4_.refs_5_.refs_6_.refs_7_.f_ref, bf16[16,64,256]{2,1,0:T(8,128)(2,1)} %get-tuple-element.195.refs_12_.refs_0_, bf16[16,64,256]{2,1,0:T(8,128)(2,1)} %copy-done.19, ...), custom_call_target="tpu_custom_call" | custom-call | flops 83886080 | bytes 20971520 | tf_op jit(solution)/shard_map/pallas_call | solution.py:263
  968.9 40.7 %shard_map.85.refs_8_ = f32[8,128,64,256]{3,2,1,0:T(8,128)} custom-call(s32[4]{0:T(128)} %pad_add_fusion.s_ref, f32[8,128,64,256]{3,2,1,0:T(8,128)} %bitcast.4.refs_0_.refs_1_.refs_2_.refs_3_.refs_4_.refs_5_.refs_6_.refs_7_.f_ref, bf16[48,64,256]{2,1,0:T(8,128)(2,1)} %get-tuple-element.215.refs_0_, ...), custom_call_target="tpu_custom_call", output_to_operand_aliasing={{}: (10, {})} | custom-call | flops 251658240 | bytes 62914560 | tf_op jit(solution)/shard_map/pallas_call | solution.py:263
  1009.6 28.0 %shard_map.86.refs_8_ = f32[8,128,64,256]{3,2,1,0:T(8,128)} custom-call(s32[4]{0:T(128)} %pad_add_fusion.s_ref, f32[8,128,64,256]{3,2,1,0:T(8,128)} %bitcast.4.refs_0_.refs_1_.refs_2_.refs_3_.refs_4_.refs_5_.refs_6_.refs_7_.f_ref, bf16[32,64,256]{2,1,0:T(8,128)(2,1)} %get-tuple-element.206.refs_0_, ...), custom_call_target="tpu_custom_call", output_to_operand_aliasing={{}: (10, {})} | custom-call | flops 167772160 | bytes 41943040 | tf_op jit(solution)/shard_map/pallas_call | solution.py:263
  1041.1 15.2 %shard_map.87 = f32[8,128,64,256]{3,2,1,0:T(8,128)} custom-call(s32[4]{0:T(128)} %pad_add_fusion.s_ref, f32[8,128,64,256]{3,2,1,0:T(8,128)} %bitcast.4.refs_0_.refs_1_.refs_2_.refs_3_.refs_4_.refs_5_.refs_6_.refs_7_.f_ref, bf16[16,64,256]{2,1,0:T(8,128)(2,1)} %get-tuple-element.197.refs_0_, ...), custom_call_target="tpu_custom_call", output_to_operand_aliasing={{}: (10, {})} | custom-call | flops 83886080 | bytes 20971520 | tf_op jit(solution)/shard_map/pallas_call | solution.py:263
  1071.1 16.1 %collective-permute-done.83 = bf16[16,64,256]{2,1,0:T(8,128)(2,1)S(1)} collective-permute-done((bf16[16,64,256]{2,1,0:T(8,128)(2,1)S(1)}, bf16[16,64,256]{2,1,0:T(8,128)(2,1)S(1)}, u32[]{:S(2)}, u32[]{:S(2)}) %collective-permute-start.83) | collective-permute-done | bytes 524320 | tf_op jit(solution)/shard_map/ppermute | solution.py:292
  (273 shorter events, 233.7 us)
Async XLA Ops:
  103.1 66.7 %collective-permute-start.10 = (bf16[48,64,256]{2,1,0:T(8,128)(2,1)}, bf16[48,64,256]{2,1,0:T(8,128)(2,1)S(1)}, u32[]{:S(2)}, u32[]{:S(2)}) collective-permute-start(bf16[48,64,256]{2,1,0:T(8,128)(2,1)} %get-tuple-element.134), channel_id=1, source_target_pairs={{0,4},{1,5},{2,6},{3,7},{4,0},{5,1},{6,2},{7,3}} | collective-permute-start | bytes 4718600 | tf_op jit(solution)/shard_map/ppermute | solution.py:292
  113.4 133.6 %collective-permute-start.11 = (bf16[48,64,256]{2,1,0:T(8,128)(2,1)}, bf16[48,64,256]{2,1,0:T(8,128)(2,1)S(1)}, u32[]{:S(2)}, u32[]{:S(2)}) collective-permute-start(bf16[48,64,256]{2,1,0:T(8,128)(2,1)} %get-tuple-element.135), channel_id=1, source_target_pairs={{0,5},{1,4},{2,7},{3,6},{4,1},{5,0},{6,3},{7,2}} | collective-permute-start | bytes 4718600 | tf_op jit(solution)/shard_map/ppermute | solution.py:292
  166.7 116.7 %collective-permute-start.12 = (bf16[48,64,256]{2,1,0:T(8,128)(2,1)}, bf16[48,64,256]{2,1,0:T(8,128)(2,1)S(1)}, u32[]{:S(2)}, u32[]{:S(2)}) collective-permute-start(bf16[48,64,256]{2,1,0:T(8,128)(2,1)} %get-tuple-element.136), channel_id=1, source_target_pairs={{0,6},{1,7},{2,4},{3,5},{4,2},{5,3},{6,0},{7,1}} | collective-permute-start | bytes 4718600 | tf_op jit(solution)/shard_map/ppermute | solution.py:292
  167.1 116.9 %collective-permute-start.13 = (bf16[48,64,256]{2,1,0:T(8,128)(2,1)}, bf16[48,64,256]{2,1,0:T(8,128)(2,1)}, u32[]{:S(2)}, u32[]{:S(2)}) collective-permute-start(bf16[48,64,256]{2,1,0:T(8,128)(2,1)} %get-tuple-element.137), channel_id=1, source_target_pairs={{0,7},{1,6},{2,5},{3,4},{4,3},{5,2},{6,1},{7,0}} | collective-permute-start | bytes 4718600 | tf_op jit(solution)/shard_map/ppermute | solution.py:292
  168.9 116.6 %collective-permute-start.7 = (bf16[48,64,256]{2,1,0:T(8,128)(2,1)}, bf16[48,64,256]{2,1,0:T(8,128)(2,1)}, u32[]{:S(2)}, u32[]{:S(2)}) collective-permute-start(bf16[48,64,256]{2,1,0:T(8,128)(2,1)} %get-tuple-element.131), channel_id=1, source_target_pairs={{0,1},{1,0},{2,3},{3,2},{4,5},{5,4},{6,7},{7,6}} | collective-permute-start | bytes 4718600 | tf_op jit(solution)/shard_map/ppermute | solution.py:292
  169.8 116.3 %collective-permute-start.8 = (bf16[48,64,256]{2,1,0:T(8,128)(2,1)}, bf16[48,64,256]{2,1,0:T(8,128)(2,1)}, u32[]{:S(2)}, u32[]{:S(2)}) collective-permute-start(bf16[48,64,256]{2,1,0:T(8,128)(2,1)} %get-tuple-element.132), channel_id=1, source_target_pairs={{0,2},{1,3},{2,0},{3,1},{4,6},{5,7},{6,4},{7,5}} | collective-permute-start | bytes 4718600 | tf_op jit(solution)/shard_map/ppermute | solution.py:292
  247.0 56.4 %collective-permute-start.9 = (bf16[48,64,256]{2,1,0:T(8,128)(2,1)}, bf16[48,64,256]{2,1,0:T(8,128)(2,1)}, u32[]{:S(2)}, u32[]{:S(2)}) collective-permute-start(bf16[48,64,256]{2,1,0:T(8,128)(2,1)} %get-tuple-element.133), channel_id=1, source_target_pairs={{0,3},{1,2},{2,1},{3,0},{4,7},{5,6},{6,5},{7,4}} | collective-permute-start | bytes 4718600 | tf_op jit(solution)/shard_map/ppermute | solution.py:292
  283.4 72.9 %collective-permute-start.16 = (bf16[32,64,256]{2,1,0:T(8,128)(2,1)}, bf16[32,64,256]{2,1,0:T(8,128)(2,1)}, u32[]{:S(2)}, u32[]{:S(2)}) collective-permute-start(bf16[32,64,256]{2,1,0:T(8,128)(2,1)} %get-tuple-element.142), channel_id=1, source_target_pairs={{0,3},{1,2},{2,1},{3,0},{4,7},{5,6},{6,5},{7,4}} | collective-permute-start | bytes 3145736 | tf_op jit(solution)/shard_map/ppermute | solution.py:292
  284.0 72.4 %collective-permute-start.17 = (bf16[32,64,256]{2,1,0:T(8,128)(2,1)S(1)}, bf16[32,64,256]{2,1,0:T(8,128)(2,1)}, u32[]{:S(2)}, u32[]{:S(2)}) collective-permute-start(bf16[32,64,256]{2,1,0:T(8,128)(2,1)S(1)} %copy-done.32), channel_id=1, source_target_pairs={{0,4},{1,5},{2,6},{3,7},{4,0},{5,1},{6,2},{7,3}} | collective-permute-start | bytes 3145736 | tf_op jit(solution)/shard_map/ppermute | solution.py:292
  285.6 91.5 %collective-permute-start.18 = (bf16[32,64,256]{2,1,0:T(8,128)(2,1)S(1)}, bf16[32,64,256]{2,1,0:T(8,128)(2,1)}, u32[]{:S(2)}, u32[]{:S(2)}) collective-permute-start(bf16[32,64,256]{2,1,0:T(8,128)(2,1)S(1)} %copy-done.31), channel_id=1, source_target_pairs={{0,5},{1,4},{2,7},{3,6},{4,1},{5,0},{6,3},{7,2}} | collective-permute-start | bytes 3145736 | tf_op jit(solution)/shard_map/ppermute | solution.py:292
  286.1 92.7 %collective-permute-start.19 = (bf16[32,64,256]{2,1,0:T(8,128)(2,1)S(1)}, bf16[32,64,256]{2,1,0:T(8,128)(2,1)}, u32[]{:S(2)}, u32[]{:S(2)}) collective-permute-start(bf16[32,64,256]{2,1,0:T(8,128)(2,1)S(1)} %copy-done.30), channel_id=1, source_target_pairs={{0,6},{1,7},{2,4},{3,5},{4,2},{5,3},{6,0},{7,1}} | collective-permute-start | bytes 3145736 | tf_op jit(solution)/shard_map/ppermute | solution.py:292
  303.4 76.5 %collective-permute-start.20 = (bf16[32,64,256]{2,1,0:T(8,128)(2,1)S(1)}, bf16[32,64,256]{2,1,0:T(8,128)(2,1)}, u32[]{:S(2)}, u32[]{:S(2)}) collective-permute-start(bf16[32,64,256]{2,1,0:T(8,128)(2,1)S(1)} %copy-done.29), channel_id=1, source_target_pairs={{0,7},{1,6},{2,5},{3,4},{4,3},{5,2},{6,1},{7,0}} | collective-permute-start | bytes 3145736 | tf_op jit(solution)/shard_map/ppermute | solution.py:292
  459.8 59.2 %collective-permute-start.36 = (bf16[128,32,128]{2,1,0:T(8,128)(2,1)}, bf16[128,32,128]{2,1,0:T(8,128)(2,1)}, u32[]{:S(2)}, u32[]{:S(2)}) collective-permute-start(bf16[128,32,128]{2,1,0:T(8,128)(2,1)} %get-tuple-element.166), channel_id=1, source_target_pairs={{0,1},{1,0},{2,3},{3,2},{4,5},{5,4},{6,7},{7,6}} | collective-permute-start | bytes 3145736 | tf_op jit(solution)/shard_map/ppermute | solution.py:292
  589.7 61.1 %collective-permute-start.76 = (bf16[16,64,256]{2,1,0:T(8,128)(2,1)}, bf16[16,64,256]{2,1,0:T(8,128)(2,1)}, u32[]{:S(2)}, u32[]{:S(2)}) collective-permute-start(bf16[16,64,256]{2,1,0:T(8,128)(2,1)} %get-tuple-element.227), channel_id=1, source_target_pairs={{0,5},{1,4},{2,7},{3,6},{4,1},{5,0},{6,3},{7,2}} | collective-permute-start | bytes 1572872 | tf_op jit(solution)/shard_map/ppermute | solution.py:292
  650.8 69.4 %collective-permute-start.58 = (bf16[32,64,256]{2,1,0:T(8,128)(2,1)}, bf16[32,64,256]{2,1,0:T(8,128)(2,1)S(1)}, u32[]{:S(2)}, u32[]{:S(2)}) collective-permute-start(bf16[32,64,256]{2,1,0:T(8,128)(2,1)} %get-tuple-element.207), channel_id=1, source_target_pairs={{0,1},{1,0},{2,3},{3,2},{4,5},{5,4},{6,7},{7,6}} | collective-permute-start | bytes 3145736 | tf_op jit(solution)/shard_map/ppermute | solution.py:292
  651.7 68.8 %collective-permute-start.59 = (bf16[32,64,256]{2,1,0:T(8,128)(2,1)}, bf16[32,64,256]{2,1,0:T(8,128)(2,1)S(1)}, u32[]{:S(2)}, u32[]{:S(2)}) collective-permute-start(bf16[32,64,256]{2,1,0:T(8,128)(2,1)} %get-tuple-element.208), channel_id=1, source_target_pairs={{0,2},{1,3},{2,0},{3,1},{4,6},{5,7},{6,4},{7,5}} | collective-permute-start | bytes 3145736 | tf_op jit(solution)/shard_map/ppermute | solution.py:292
  653.2 68.0 %collective-permute-start.60 = (bf16[32,64,256]{2,1,0:T(8,128)(2,1)}, bf16[32,64,256]{2,1,0:T(8,128)(2,1)}, u32[]{:S(2)}, u32[]{:S(2)}) collective-permute-start(bf16[32,64,256]{2,1,0:T(8,128)(2,1)} %get-tuple-element.209), channel_id=1, source_target_pairs={{0,3},{1,2},{2,1},{3,0},{4,7},{5,6},{6,5},{7,4}} | collective-permute-start | bytes 3145736 | tf_op jit(solution)/shard_map/ppermute | solution.py:292
  654.2 68.9 %collective-permute-start.61 = (bf16[32,64,256]{2,1,0:T(8,128)(2,1)}, bf16[32,64,256]{2,1,0:T(8,128)(2,1)}, u32[]{:S(2)}, u32[]{:S(2)}) collective-permute-start(bf16[32,64,256]{2,1,0:T(8,128)(2,1)} %get-tuple-element.210), channel_id=1, source_target_pairs={{0,4},{1,5},{2,6},{3,7},{4,0},{5,1},{6,2},{7,3}} | collective-permute-start | bytes 3145736 | tf_op jit(solution)/shard_map/ppermute | solution.py:292
  719.8 83.7 %collective-permute-start.65 = (bf16[48,64,256]{2,1,0:T(8,128)(2,1)}, bf16[48,64,256]{2,1,0:T(8,128)(2,1)S(1)}, u32[]{:S(2)}, u32[]{:S(2)}) collective-permute-start(bf16[48,64,256]{2,1,0:T(8,128)(2,1)} %get-tuple-element.216), channel_id=1, source_target_pairs={{0,1},{1,0},{2,3},{3,2},{4,5},{5,4},{6,7},{7,6}} | collective-permute-start | bytes 4718600 | tf_op jit(solution)/shard_map/ppermute | solution.py:292
  720.1 84.3 %collective-permute-start.66 = (bf16[48,64,256]{2,1,0:T(8,128)(2,1)}, bf16[48,64,256]{2,1,0:T(8,128)(2,1)S(1)}, u32[]{:S(2)}, u32[]{:S(2)}) collective-permute-start(bf16[48,64,256]{2,1,0:T(8,128)(2,1)} %get-tuple-element.217), channel_id=1, source_target_pairs={{0,2},{1,3},{2,0},{3,1},{4,6},{5,7},{6,4},{7,5}} | collective-permute-start | bytes 4718600 | tf_op jit(solution)/shard_map/ppermute | solution.py:292
  721.1 59.7 %collective-permute-start.63 = (bf16[32,64,256]{2,1,0:T(8,128)(2,1)}, bf16[32,64,256]{2,1,0:T(8,128)(2,1)S(1)}, u32[]{:S(2)}, u32[]{:S(2)}) collective-permute-start(bf16[32,64,256]{2,1,0:T(8,128)(2,1)} %get-tuple-element.212), channel_id=1, source_target_pairs={{0,6},{1,7},{2,4},{3,5},{4,2},{5,3},{6,0},{7,1}} | collective-permute-start | bytes 3145736 | tf_op jit(solution)/shard_map/ppermute | solution.py:292
  723.1 78.4 %collective-permute-start.64 = (bf16[32,64,256]{2,1,0:T(8,128)(2,1)}, bf16[32,64,256]{2,1,0:T(8,128)(2,1)S(1)}, u32[]{:S(2)}, u32[]{:S(2)}) collective-permute-start(bf16[32,64,256]{2,1,0:T(8,128)(2,1)} %get-tuple-element.213), channel_id=1, source_target_pairs={{0,7},{1,6},{2,5},{3,4},{4,3},{5,2},{6,1},{7,0}} | collective-permute-start | bytes 3145736 | tf_op jit(solution)/shard_map/ppermute | solution.py:292
  746.0 88.8 %collective-permute-start.67 = (bf16[48,64,256]{2,1,0:T(8,128)(2,1)}, bf16[48,64,256]{2,1,0:T(8,128)(2,1)}, u32[]{:S(2)}, u32[]{:S(2)}) collective-permute-start(bf16[48,64,256]{2,1,0:T(8,128)(2,1)} %get-tuple-element.218), channel_id=1, source_target_pairs={{0,3},{1,2},{2,1},{3,0},{4,7},{5,6},{6,5},{7,4}} | collective-permute-start | bytes 4718600 | tf_op jit(solution)/shard_map/ppermute | solution.py:292
  780.8 56.4 %collective-permute-start.68 = (bf16[48,64,256]{2,1,0:T(8,128)(2,1)}, bf16[48,64,256]{2,1,0:T(8,128)(2,1)}, u32[]{:S(2)}, u32[]{:S(2)}) collective-permute-start(bf16[48,64,256]{2,1,0:T(8,128)(2,1)} %get-tuple-element.219), channel_id=1, source_target_pairs={{0,4},{1,5},{2,6},{3,7},{4,0},{5,1},{6,2},{7,3}} | collective-permute-start | bytes 4718600 | tf_op jit(solution)/shard_map/ppermute | solution.py:292
  801.5 135.7 %collective-permute-start.69 = (bf16[48,64,256]{2,1,0:T(8,128)(2,1)}, bf16[48,64,256]{2,1,0:T(8,128)(2,1)}, u32[]{:S(2)}, u32[]{:S(2)}) collective-permute-start(bf16[48,64,256]{2,1,0:T(8,128)(2,1)} %get-tuple-element.220), channel_id=1, source_target_pairs={{0,5},{1,4},{2,7},{3,6},{4,1},{5,0},{6,3},{7,2}} | collective-permute-start | bytes 4718600 | tf_op jit(solution)/shard_map/ppermute | solution.py:292
  803.5 134.3 %collective-permute-start.70 = (bf16[48,64,256]{2,1,0:T(8,128)(2,1)}, bf16[48,64,256]{2,1,0:T(8,128)(2,1)}, u32[]{:S(2)}, u32[]{:S(2)}) collective-permute-start(bf16[48,64,256]{2,1,0:T(8,128)(2,1)} %get-tuple-element.221), channel_id=1, source_target_pairs={{0,6},{1,7},{2,4},{3,5},{4,2},{5,3},{6,0},{7,1}} | collective-permute-start | bytes 4718600 | tf_op jit(solution)/shard_map/ppermute | solution.py:292
  804.5 147.4 %collective-permute-start.71 = (bf16[48,64,256]{2,1,0:T(8,128)(2,1)}, bf16[48,64,256]{2,1,0:T(8,128)(2,1)S(1)}, u32[]{:S(2)}, u32[]{:S(2)}) collective-permute-start(bf16[48,64,256]{2,1,0:T(8,128)(2,1)} %get-tuple-element.222), channel_id=1, source_target_pairs={{0,7},{1,6},{2,5},{3,4},{4,3},{5,2},{6,1},{7,0}} | collective-permute-start | bytes 4718600 | tf_op jit(solution)/shard_map/ppermute | solution.py:292
  834.8 202.8 %collective-permute-start.54 = (bf16[16,64,256]{2,1,0:T(8,128)(2,1)}, bf16[16,64,256]{2,1,0:T(8,128)(2,1)}, u32[]{:S(2)}, u32[]{:S(2)}) collective-permute-start(bf16[16,64,256]{2,1,0:T(8,128)(2,1)} %get-tuple-element.201), channel_id=1, source_target_pairs={{0,4},{1,5},{2,6},{3,7},{4,0},{5,1},{6,2},{7,3}} | collective-permute-start | bytes 1572872 | tf_op jit(solution)/shard_map/ppermute | solution.py:292
  837.2 200.7 %collective-permute-start.55 = (bf16[16,64,256]{2,1,0:T(8,128)(2,1)}, bf16[16,64,256]{2,1,0:T(8,128)(2,1)}, u32[]{:S(2)}, u32[]{:S(2)}) collective-permute-start(bf16[16,64,256]{2,1,0:T(8,128)(2,1)} %get-tuple-element.202), channel_id=1, source_target_pairs={{0,5},{1,4},{2,7},{3,6},{4,1},{5,0},{6,3},{7,2}} | collective-permute-start | bytes 1572872 | tf_op jit(solution)/shard_map/ppermute | solution.py:292
  937.2 101.8 %collective-permute-start.56 = (bf16[16,64,256]{2,1,0:T(8,128)(2,1)}, bf16[16,64,256]{2,1,0:T(8,128)(2,1)}, u32[]{:S(2)}, u32[]{:S(2)}) collective-permute-start(bf16[16,64,256]{2,1,0:T(8,128)(2,1)} %get-tuple-element.203), channel_id=1, source_target_pairs={{0,6},{1,7},{2,4},{3,5},{4,2},{5,3},{6,0},{7,1}} | collective-permute-start | bytes 1572872 | tf_op jit(solution)/shard_map/ppermute | solution.py:292
  937.8 102.1 %collective-permute-start.57 = (bf16[16,64,256]{2,1,0:T(8,128)(2,1)}, bf16[16,64,256]{2,1,0:T(8,128)(2,1)}, u32[]{:S(2)}, u32[]{:S(2)}) collective-permute-start(bf16[16,64,256]{2,1,0:T(8,128)(2,1)} %get-tuple-element.204), channel_id=1, source_target_pairs={{0,7},{1,6},{2,5},{3,4},{4,3},{5,2},{6,1},{7,0}} | collective-permute-start | bytes 1572872 | tf_op jit(solution)/shard_map/ppermute | solution.py:292
  953.1 105.7 %collective-permute-start.79 = (bf16[16,64,256]{2,1,0:T(8,128)(2,1)}, bf16[16,64,256]{2,1,0:T(8,128)(2,1)}, u32[]{:S(2)}, u32[]{:S(2)}) collective-permute-start(bf16[16,64,256]{2,1,0:T(8,128)(2,1)} %get-tuple-element.232), channel_id=1, source_target_pairs={{0,1},{1,0},{2,3},{3,2},{4,5},{5,4},{6,7},{7,6}} | collective-permute-start | bytes 1572872 | tf_op jit(solution)/shard_map/ppermute | solution.py:292
  (102 other events, 3440.4 us)
where the time goes:
time: 1100 us; the launch traced here: 1090 us
  Pallas kernels  470 us (43%)
  waiting for transfers between devices  446 us (41%)
  local copies, waits for them, and re-layouts  80.5 us (7%)
  starting transfers between devices  77.8 us (7%)
  other arithmetic  20.4 us (2%)
    pallas_call x25, Pallas kernels, call(): return lambda *args: fn(*args, *deps)  470 us
    ppermute x86, waiting for transfers between devices, swap(): return lax.ppermute(x, ('lon', 'lat'), [(s, s ^ t) for s in range(nd)])  446 us
    ppermute x86, starting transfers between devices, swap(): return lax.ppermute(x, ('lon', 'lat'), [(s, s ^ t) for s in range(nd)])  77.8 us
    unnamed x97, local copies, waits for them, and re-layouts  30.8 us
    dynamic_slice x1, local copies, waits for them, and re-layouts, local_layer(): lax.dynamic_index_in_dim(w, h, axis=1, keepdims=False)  26.7 us
    squeeze x1, local copies, waits for them, and re-layouts, local_layer(): w_re, w_im = (w[..., 0], w[..., 1])  23 us
  transfers between devices with their start and end apart: 86, of which 22 were waited for; matrix products, arithmetic and copies ran while one was open for 8% of the time, Pallas kernels for 39%

commit v1 on v0

--- a/solution.py
+++ b/solution.py
@@ -13,7 +13,8 @@
 F32 = jnp.float32
 LB = 16
 HALVES = ((16, 48), (32, 16, 16))
-MB = 16
+MB = 32
+PAD = LB + 1
 MG = 64
 NV = 4
 NT = (((1,), (1,)), ((), ()))
@@ -64,7 +65,7 @@
 def cast_kernel(s_ref, *refs):
     n = len(refs) // 2
     for t in range(n):
-        refs[n + t][...] = refs[t][0].astype(BF)
+        refs[n + t][...] = refs[t][0, 0, 0].astype(BF)
 
 
 def fwd_dft_kernel(s_ref, tab_ref, *refs):
@@ -85,15 +86,15 @@
             c = c2 * 2 + u
             res = lax.dot_general(tab_ref[0], rc[u], NT, preferred_element_type=F32)
             for j in range(res.shape[1] // 128):
-                scr[j, pl.ds(c, nms, stride=16), :] = res[:, j * 128:(j + 1) * 128]
+                scr[j, pl.ds(c, nms, stride=PAD), :] = res[:, j * 128:(j + 1) * 128]
         return carry
 
     lax.fori_loop(0, 8, body, 0)
 
     def flush(i, carry):
         for j in range(scr.shape[0]):
-            blk = scr[j, pl.ds(pl.multiple_of(i * 512, 512), 512), :]
-            out[pl.ds(i * 32, 32), :, j * 128:(j + 1) * 128] = blk.reshape(32, 16, 128).astype(BF)
+            for u in range(32):
+                out[i * 32 + u, :, j * 128:(j + 1) * 128] = scr[j, pl.ds((i * 32 + u) * PAD, LB), :].astype(BF)
         return carry
 
     lax.fori_loop(0, nms // 32, flush, 0)
@@ -124,7 +125,7 @@
 
 def mix_kernel(vs, s_ref, wre, wim, *refs):
     ins = {v: refs[4 * n:4 * n + 4] for n, v in enumerate(vs)}
-    outs = {v: refs[8 + 4 * n:12 + 4 * n] for n, v in enumerate(vs)}
+    outs = {v: refs[8 + 2 * n:10 + 2 * n] for n, v in enumerate(vs)}
     scr_a, scr_b = refs[-2:]
     h = s_ref[3]
     for n, v in enumerate(vs):
@@ -133,44 +134,44 @@
             nm = MG * (v + 1)
 
             def fill(i, carry):
-                rows = pl.ds(pl.multiple_of(i * 512, 512), 512)
-                for half in range(2):
-                    scr_a[2 * h + half, rows, :] = ins[v][half][pl.ds(i * 32, 32)].astype(F32).reshape(512, 128)
-                    scr_a[2 - 2 * h + half, rows, :] = ins[v][2 + half][pl.ds(i * 32, 32)].astype(F32).reshape(512, 128)
+                for u in range(16):
+                    rows = pl.ds((i * 16 + u) * PAD, LB)
+                    for half in range(2):
+                        scr_a[2 * half + h, rows, :] = ins[v][half][i * 16 + u].astype(F32)
+                        scr_a[2 * half + 1 - h, rows, :] = ins[v][2 + half][i * 16 + u].astype(F32)
                 return carry
 
-            lax.fori_loop(0, nm // 32, fill, 0)
+            lax.fori_loop(0, nm // 16, fill, 0)
 
             def body(li2, carry):
                 for u in range(2):
                     li = li2 * 2 + u
-                    lhs = jnp.concatenate([scr_a[b, pl.ds(li, nm, stride=LB), :].astype(BF) for b in range(4)], axis=1)
+                    lhs = jnp.concatenate([scr_a[b, pl.ds(li, nm, stride=PAD), :].astype(BF) for b in range(4)], axis=1)
                     wr, wi = wre[li], wim[li]
                     ni = -wi
                     cg = wr.shape[0] // 4
-                    rhs_re = jnp.concatenate([w[b * cg:(b + 1) * cg] for b in range(4) for w in (wr, ni)], axis=0)
-                    rhs_im = jnp.concatenate([w[b * cg:(b + 1) * cg] for b in range(4) for w in (wi, wr)], axis=0)
-                    bre = jnp.dot(lhs, rhs_re, preferred_element_type=F32)
-                    bim = jnp.dot(lhs, rhs_im, preferred_element_type=F32)
+                    rhs = jnp.concatenate([jnp.concatenate([w[b * cg:(b + 1) * cg] for b in range(4) for w in pair], axis=0)
+                                           for pair in ((wr, ni), (wi, wr))], axis=1)
+                    res = jnp.dot(lhs, rhs, preferred_element_type=F32)
                     for b in range(2):
-                        scr_b[b, pl.ds(li, nm, stride=LB), :] = bre[:, b * 128:(b + 1) * 128]
-                        scr_b[2 + b, pl.ds(li, nm, stride=LB), :] = bim[:, b * 128:(b + 1) * 128]
+                        scr_b[b, pl.ds(li, nm, stride=PAD), :] = res[:, b * 128:(b + 1) * 128]
                 return carry
 
             lax.fori_loop(0, LB // 2, body, 0)
-            low = lax.broadcasted_iota(jnp.int32, (512, 128), 1) < 64
+            low = lax.broadcasted_iota(jnp.int32, (LB, 128), 1) < 64
+            first_is_mine = h == 0
 
             def flush(i, carry):
-                rows = pl.ds(pl.multiple_of(i * 512, 512), 512)
-                for side, hh in ((0, h), (2, 1 - h)):
-                    re, im = scr_b[hh, rows, :], scr_b[2 + hh, rows, :]
-                    first = jnp.where(low, re, pltpu.roll(im, 64, 1))
-                    second = jnp.where(low, pltpu.roll(re, 64, 1), im)
-                    outs[v][side][pl.ds(i * 32, 32)] = first.reshape(32, LB, 128).astype(BF)
-                    outs[v][side + 1][pl.ds(i * 32, 32)] = second.reshape(32, LB, 128).astype(BF)
+                for u in range(16):
+                    rows = pl.ds((i * 16 + u) * PAD, LB)
+                    re, im = scr_b[0, rows, :], scr_b[1, rows, :]
+                    zero = jnp.where(low, re, pltpu.roll(im, 64, 1))
+                    one = jnp.where(low, pltpu.roll(re, 64, 1), im)
+                    outs[v][0][i * 16 + u] = jnp.where(first_is_mine, zero, one).astype(BF)
+                    outs[v][1][i * 16 + u] = jnp.where(first_is_mine, one, zero).astype(BF)
                 return carry
 
-            lax.fori_loop(0, nm // 32, flush, 0)
+            lax.fori_loop(0, nm // 16, flush, 0)
 
 
 def inv_leg_kernel(no, s_ref, *refs):
@@ -207,8 +208,8 @@
 
     def fill(i, carry):
         for j in range(scr.shape[0]):
-            blk = g_ref[pl.ds(i * 32, 32), :, j * 128:(j + 1) * 128].astype(F32)
-            scr[j, pl.ds(pl.multiple_of(i * 512, 512), 512), :] = blk.reshape(512, 128)
+            for u in range(32):
+                scr[j, pl.ds((i * 32 + u) * PAD, LB), :] = g_ref[i * 32 + u, :, j * 128:(j + 1) * 128].astype(F32)
         return carry
 
     lax.fori_loop(0, nms // 32, fill, 0)
@@ -216,7 +217,7 @@
     def body(c2, carry):
         for u in range(2):
             c = c2 * 2 + u
-            g = jnp.concatenate([scr[j, pl.ds(c, nms, stride=16), :].astype(BF) for j in range(scr.shape[0])], axis=1)
+            g = jnp.concatenate([scr[j, pl.ds(c, nms, stride=PAD), :].astype(BF) for j in range(scr.shape[0])], axis=1)
             yc[u] = lax.dot_general(g, tab_ref[0], TN, preferred_element_type=F32).astype(BF)
         for u in range(2):
             c = c2 * 2 + u
@@ -242,7 +243,7 @@
             buf[...] = pieces[n][...]
 
     def body(c, carry):
-        out[0, c] = f_ref[0, c] + gelu(buf[c].astype(F32))
+        out[0, 0, 0, c] = f_ref[0, 0, 0, c] + gelu(buf[c].astype(F32))
         return carry
 
     lax.fori_loop(0, buf.shape[0], body, 0)
@@ -284,7 +285,7 @@
         pw_np, pi_np = legendre_tables(n_lat, n_lon, n_deg)
         tf_np, ti_np = dft_tables(n_lon, n_deg)
         pw, pi, tf, ti = jnp.asarray(pw_np), jnp.asarray(pi_np), jnp.asarray(tf_np), jnp.asarray(ti_np)
-        f8 = grid_field.reshape(nd, half_c, row_count, col_count)
+        f6 = grid_field.reshape(batch, 2, channels // half_c, half_c // 2, row_count, col_count)
 
         def swap(x, t):
             if t == 0:
@@ -296,16 +297,17 @@
 
         tab_spec = pl.BlockSpec((1, nms, n_lon), lambda i, s: (s[1], 0, 0))
         piece_spec16 = pl.BlockSpec((16, row_count, col_count), lambda i, s: (i, 0, 0))
-        dft_scratch = [pltpu.VMEM((n_lat // 128, nms * 16, 128), F32), pltpu.VMEM((2, n_lat, n_lon), BF)]
-
-        def cast_chunk(c0, cc):
+        dft_scratch = [pltpu.VMEM((n_lat // 128, nms * PAD, 128), F32), pltpu.VMEM((2, n_lat, n_lon), BF)]
+
+        def cast_chunk(half, c0, cc):
             cb = 8
             base = c0 // cb
             return call(
                 cast_kernel, (cc // cb,),
-                [pl.BlockSpec((1, cb, row_count, col_count), functools.partial(lambda t, i, s: (s[0] ^ t, base + i, 0, 0), t)) for t in range(nd)],
+                [pl.BlockSpec((1, 1, 1, cb, row_count, col_count),
+                              functools.partial(lambda t, i, s: ((s[0] ^ t) // 2, half, (s[0] ^ t) % 2, base + i, 0, 0), t)) for t in range(nd)],
                 [pl.BlockSpec((cb, row_count, col_count), lambda i, s: (i, 0, 0))] * nd,
-                [piece(cc)] * nd, 1e6, nd * cc * row_count * col_count * 6)(scal, *([f8] * nd))
+                [piece(cc)] * nd, 1e6, nd * cc * row_count * col_count * 6)(scal, *([f6] * nd))
 
         def dft_chunk(pieces, cc, deps):
             return call(
@@ -340,11 +342,11 @@
                 1.3 * n_deg * n_deg * n_lat * half_c, 50e6, (), deps)(scal, *([pi] * NV), *mine, *recv)
 
         sizes = HALVES[0] + HALVES[1]
-        starts = [sum(sizes[:k]) for k in range(len(sizes))]
+        starts = [(half, sum(part[:k])) for half, part in enumerate(HALVES) for k in range(len(part))]
         recv = []
-        for c0, cc in zip(starts, sizes):
+        for (half, c0), cc in zip(starts, sizes):
             k = len(recv)
-            pieces = cast_chunk(c0, cc)
+            pieces = cast_chunk(half, c0, cc)
             recv.append([swap(p, t) for t, p in enumerate(pieces)])
 
         w = mix_weight.reshape(n_deg // (2 * LB), 2, LB, channels, channels, 2)
@@ -371,29 +373,31 @@
                 got[v] = swap(send[v], 1)
             a_recv.append(got)
 
-        def mix(vs):
+        def mix(vs, out_half):
             first = vs[0] * 2
             jump = [lambda j: jnp.minimum(j, 1), lambda j: jnp.maximum(j - 2, 0)]
-            w_spec = pl.BlockSpec((LB, channels, channels), lambda j, s: (jnp.where(j < 2, first + j, first + j - 4), 0, 0))
-            specs, shapes, args = [], [], []
+            w_spec = pl.BlockSpec((LB, channels, channels // 2), lambda j, s: (jnp.where(j < 2, first + j, first + j - 4), 0, out_half))
+            specs, outs, shapes, args = [], [], [], []
             for n, v in enumerate(vs):
-                specs += [pl.BlockSpec((MG * (v + 1), LB, half_c), functools.partial(lambda n, j, s: (0, jump[n](j), 0), n))] * 4
-                shapes += [spec_shapes[v]] * 4
+                spec = pl.BlockSpec((MG * (v + 1), LB, half_c), functools.partial(lambda n, j, s: (0, jump[n](j), 0), n))
+                specs += [spec] * 4
+                outs += [spec] * 2
+                shapes += [spec_shapes[v]] * 2
                 args += [a_mine[0][v], a_mine[1][v], a_recv[0][v], a_recv[1][v]]
-            rows = MG * (vs[0] + 1) * LB
-            return call(
-                functools.partial(mix_kernel, vs), (4,), [w_spec, w_spec] + specs, specs, shapes,
-                8.0 * 4 * LB * MG * (vs[0] + 1) * channels * channels, 60e6,
-                [pltpu.VMEM((4, rows, 128), F32), pltpu.VMEM((4, rows, 128), F32)])(scal, w_re, w_im, *args)
-
-        b_mine = [[None] * NV, [None] * NV]
-        b_recv = [[None] * NV, [None] * NV]
-        for vs in ((3, 2), (1, 0)):
-            res = mix(vs)
-            for n, v in enumerate(vs):
-                for half in range(2):
-                    b_mine[half][v] = res[4 * n + half]
-                    b_recv[half][v] = swap(res[4 * n + 2 + half], 1)
+            rows = MG * (vs[0] + 1) * PAD
+            return call(
+                functools.partial(mix_kernel, vs), (4,), [w_spec, w_spec] + specs, outs, shapes,
+                4.0 * 4 * LB * MG * (vs[0] + 1) * channels * channels, 40e6,
+                [pltpu.VMEM((4, rows, 128), F32), pltpu.VMEM((2, rows, 128), F32)])(scal, w_re, w_im, *args)
+
+        def mix_half(half):
+            mine, recv = [None] * NV, [None] * NV
+            for vs in ((3, 2), (1, 0)):
+                res = mix(vs, half)
+                for n, v in enumerate(vs):
+                    mine[v] = res[2 * n]
+                    recv[v] = swap(res[2 * n + 1], 1)
+            return mine, recv
 
         def idft_chunk(g):
             cc = g.shape[1]
@@ -403,10 +407,10 @@
                 [piece_spec16] * nd, [piece(cc)] * nd,
                 4.0 * cc * nms * n_lat * n_lon, cc * nms * n_lat * 6, dft_scratch)(scal, ti, g)
 
-        def final_chunk(c0, cc, pieces, out):
+        def final_chunk(half, c0, cc, pieces, out):
             cb = 8
             base, nb = c0 // cb, cc // cb
-            big = pl.BlockSpec((1, cb, row_count, col_count), lambda t, i, s: (s[0] ^ t, base + i, 0, 0))
+            big = pl.BlockSpec((1, 1, 1, cb, row_count, col_count), lambda t, i, s: ((s[0] ^ t) // 2, half, (s[0] ^ t) % 2, base + i, 0, 0))
 
             def own(n):
                 return pl.BlockSpec((cb, row_count, col_count),
@@ -415,28 +419,26 @@
             deps = [] if out is None else [out]
             return call(
                 final_kernel, (nd, nb), [big] + [own(n) for n in range(nd)], big,
-                jax.ShapeDtypeStruct(f8.shape, F32), 40 * nd * cc * row_count * col_count, 10 * nd * cc * row_count * col_count,
+                jax.ShapeDtypeStruct(f6.shape, F32), 40 * nd * cc * row_count * col_count, 10 * nd * cc * row_count * col_count,
                 [pltpu.VMEM((cb, row_count, col_count), BF)], deps,
-                {2 + nd: 0} if deps else None)(scal, f8, *pieces)
+                {2 + nd: 0} if deps else None)(scal, f6, *pieces)
 
         k = 0
         out = None
-        dep = ()
         for half in range(2):
-            gs = leg_inv(half, b_mine[half], b_recv[half], dep)
+            b_mine, b_recv = mix_half(half)
+            gs = leg_inv(half, b_mine, b_recv)
             for g in gs:
                 cc = g.shape[1]
                 pieces = idft_chunk(g)
-                if k == 0:
-                    dep = (pieces[0],)
                 got = [swap(p, t) for t, p in enumerate(pieces)]
                 if k < len(sizes) - 1:
-                    out = final_chunk(starts[k], cc, got, out)
+                    out = final_chunk(*starts[k], cc, got, out)
                 else:
                     for t, p in enumerate(got):
-                        src = lax.dynamic_slice(f8, (me ^ t, starts[k], 0, 0), (1, cc, row_count, col_count))
-                        new = src + gelu(p.astype(F32))[None]
-                        out = lax.dynamic_update_slice(out, new, (me ^ t, starts[k], 0, 0))
+                        at = ((me ^ t) // 2, starts[k][0], (me ^ t) % 2, starts[k][1], 0, 0)
+                        src = lax.dynamic_slice(f6, at, (1, 1, 1, cc, row_count, col_count))
+                        out = lax.dynamic_update_slice(out, src + gelu(p.astype(F32))[None, None, None], at)
                 k += 1
         return out.reshape(grid_field.shape)
 

time: 1100 us -> 1120 us (1.018)
  waiting for transfers between devices: 446 us -> 496 us
  Pallas kernels: 470 us -> 432 us
    ppermute x86, waiting for transfers between devices: 446 us -> 496 us  [swap(): return lax.ppermute(x, ('lon', 'lat'), [(s, s ^ t) for s in range(nd)])]
    pallas_call x25 -> x27, Pallas kernels: 470 us -> 432 us  [call(): return lambda *args: fn(*args, *deps)]
    unnamed x97 -> x93, local copies, waits for them, and re-layouts: 30.8 us -> 33.4 us
  transfers between devices with their start and end apart: 86 -> 86, of which waited for: 22 -> 24; matrix products, arithmetic and copies ran while one was open for 8% -> 8% of each run, Pallas kernels for 39% -> 38%
where the time goes in v1:
time: 1120 us; the launch traced here: 1110 us
  waiting for transfers between devices  496 us (44%)
  Pallas kernels  432 us (39%)
  local copies, waits for them, and re-layouts  83.5 us (7%)
  starting transfers between devices  80.5 us (7%)
  other arithmetic  20.4 us (2%)
    ppermute x86, waiting for transfers between devices, swap(): return lax.ppermute(x, ('lon', 'lat'), [(s, s ^ t) for s in range(nd)])  496 us
    pallas_call x27, Pallas kernels, call(): return lambda *args: fn(*args, *deps)  432 us
    ppermute x86, starting transfers between devices, swap(): return lax.ppermute(x, ('lon', 'lat'), [(s, s ^ t) for s in range(nd)])  80.5 us
    unnamed x93, local copies, waits for them, and re-layouts  33.4 us
    dynamic_slice x1, local copies, waits for them, and re-layouts, local_layer(): lax.dynamic_index_in_dim(w, h, axis=1, keepdims=False)  26.7 us
    squeeze x1, local copies, waits for them, and re-layouts, local_layer(): w_re, w_im = (w[..., 0], w[..., 1])  23.4 us
  transfers between devices with their start and end apart: 86, of which 24 were waited for; matrix products, arithmetic and copies ran while one was open for 8% of the time, Pallas kernels for 38%

profile of v1, /device:TPU:0, one launch (start us, length us, event | category | flops | bytes accessed | tf_op | source)
XLA Modules:
  0.0 1112.8 jit_solution(306435743584025469)
XLA Ops:
  36.4 21.1 %collective-permute-done.4.refs_5_ = bf16[16,64,256]{2,1,0:T(8,128)(2,1)} collective-permute-done((bf16[16,64,256]{2,1,0:T(8,128)(2,1)}, bf16[16,64,256]{2,1,0:T(8,128)(2,1)}, u32[]{:S(2)}, u32[]{:S(2)}) %collective-permute-start.4) | collective-permute-done | bytes 524320 | tf_op jit(solution)/shard_map/ppermute | solution.py:293
  115.4 26.7 %constant_dynamic-slice_fusion = bf16[8,1,16,256,256,2]{4,5,3,2,1,0:T(2,128)(2,1)} fusion(bf16[8,2,16,256,256,2]{4,5,3,2,1,0:T(2,128)(2,1)} %bitcast.5, s32[]{:T(128)S(6)} %select_n.133), kind=kLoop, calls=%fused_computation.66 | loop fusion | bytes 67108864 | tf_op jit(solution)/shard_map/jit(dynamic_index_in_dim)/dynamic_slice | solution.py:353
  142.1 22.7 %copy.11 = bf16[8,1,16,256,256,2]{4,3,2,0,5,1:T(8,128)(2,1)} copy(bf16[8,1,16,256,256,2]{4,5,3,2,1,0:T(2,128)(2,1)} %constant_dynamic-slice_fusion) | data formatting | bytes 67108864
  164.8 18.3 %collective-permute-done.29.refs_2_ = bf16[16,64,256]{2,1,0:T(8,128)(2,1)} collective-permute-done((bf16[16,64,256]{2,1,0:T(8,128)(2,1)}, bf16[16,64,256]{2,1,0:T(8,128)(2,1)}, u32[]{:S(2)}, u32[]{:S(2)}) %collective-permute-start.29) | collective-permute-done | bytes 524320 | tf_op jit(solution)/shard_map/ppermute | solution.py:293
  187.8 23.4 %slice_bitcast_fusion = (bf16[128,256,256]{2,1,0:T(8,128)(2,1)}, bf16[128,256,256]{2,1,0:T(8,128)(2,1)}) fusion(bf16[128,256,256,2]{2,1,0,3:T(8,128)(2,1)} %bitcast.60), kind=kLoop, calls=%fused_computation | loop fusion | bytes 67108864 | tf_op jit(solution)/shard_map/squeeze | solution.py:354
  222.6 65.2 %collective-permute-done.10.refs_4_ = bf16[48,64,256]{2,1,0:T(8,128)(2,1)} collective-permute-done((bf16[48,64,256]{2,1,0:T(8,128)(2,1)}, bf16[48,64,256]{2,1,0:T(8,128)(2,1)}, u32[]{:S(2)}, u32[]{:S(2)}) %collective-permute-start.10) | collective-permute-done | bytes 1572896 | tf_op jit(solution)/shard_map/ppermute | solution.py:293
  290.2 31.4 %collective-permute-done.11.refs_5_ = bf16[48,64,256]{2,1,0:T(8,128)(2,1)} collective-permute-done((bf16[48,64,256]{2,1,0:T(8,128)(2,1)}, bf16[48,64,256]{2,1,0:T(8,128)(2,1)}, u32[]{:S(2)}, u32[]{:S(2)}) %collective-permute-start.11) | collective-permute-done | bytes 1572896 | tf_op jit(solution)/shard_map/ppermute | solution.py:293
  325.2 19.6 %shard_map.67.refs_5_.refs_8_ = bf16[512,48,256]{2,1,0:T(8,128)(2,1)} custom-call(s32[4]{0:T(128)} %pad_add_fusion.s_ref, bf16[2,512,512]{2,1,0:T(8,128)(2,1)} %constant.148.clone.tab_ref, bf16[48,64,256]{2,1,0:T(8,128)(2,1)} %get-tuple-element.130.refs_0_, bf16[48,64,256]{2,1,0:T(8,128)(2,1)} %copy-done.10, bf16[48,64,256]{2,1,0:T(8,128)(2,1)} %copy-done.11, ...), custom_call_target="tpu_custom_call" | custom-call | flops 12884901888 | bytes 37748736 | tf_op jit(solution)/shard_map/pallas_call | solution.py:264
  344.9 21.4 %shard_map.68 = (bf16[64,32,128]{2,1,0:T(8,128)(2,1)}, bf16[128,32,128]{2,1,0:T(8,128)(2,1)}, bf16[192,32,128]{2,1,0:T(8,128)(2,1)}, bf16[256,32,128]{2,1,0:T(8,...) custom-call(s32[4]{0:T(128)} %pad_add_fusion.s_ref, ...), custom_call_target="tpu_custom_call" | custom-call | flops 2791728640 | bytes 50000000 | tf_op jit(solution)/shard_map/pallas_call | solution.py:264
  368.4 21.1 %collective-permute-done.17.refs_4_ = bf16[32,64,256]{2,1,0:T(8,128)(2,1)} collective-permute-done((bf16[32,64,256]{2,1,0:T(8,128)(2,1)S(1)}, bf16[32,64,256]{2,1,0:T(8,128)(2,1)}, u32[]{:S(2)}, u32[]{:S(2)}) %collective-permute-start.17) | collective-permute-done | bytes 1048608 | tf_op jit(solution)/shard_map/ppermute | solution.py:293
  391.3 20.2 %collective-permute-done.18.refs_5_ = bf16[32,64,256]{2,1,0:T(8,128)(2,1)} collective-permute-done((bf16[32,64,256]{2,1,0:T(8,128)(2,1)S(1)}, bf16[32,64,256]{2,1,0:T(8,128)(2,1)}, u32[]{:S(2)}, u32[]{:S(2)}) %collective-permute-start.18) | collective-permute-done | bytes 1048608 | tf_op jit(solution)/shard_map/ppermute | solution.py:293
  415.1 14.9 %shard_map.70.refs_8_.refs_4_ = bf16[512,32,256]{2,1,0:T(8,128)(2,1)} custom-call(s32[4]{0:T(128)} %pad_add_fusion.s_ref, bf16[2,512,512]{2,1,0:T(8,128)(2,1)} %constant.148.clone.tab_ref, bf16[32,64,256]{2,1,0:T(8,128)(2,1)} %get-tuple-element.139.refs_0_, bf16[32,64,256]{2,1,0:T(8,128)(2,1)} %collective-permute-done.14.refs_1_, ...), custom_call_target="tpu_custom_call" | custom-call | flops 8589934592 | bytes 25165824 | tf_op jit(solution)/shard_map/pallas_call | solution.py:264
  467.2 21.1 %shard_map.75 = (bf16[64,32,128]{2,1,0:T(8,128)(2,1)}, bf16[128,32,128]{2,1,0:T(8,128)(2,1)}, bf16[192,32,128]{2,1,0:T(8,128)(2,1)}, bf16[256,32,128]{2,1,0:T(8,...) custom-call(s32[4]{0:T(128)} %pad_add_fusion.s_ref, ...), custom_call_target="tpu_custom_call" | custom-call | flops 2791728640 | bytes 50000000 | tf_op jit(solution)/shard_map/pallas_call | solution.py:264
  497.4 24.3 %shard_map.77 = (bf16[256,32,128]{2,1,0:T(8,128)(2,1)}, bf16[256,32,128]{2,1,0:T(8,128)(2,1)}, bf16[192,32,128]{2,1,0:T(8,128)(2,1)}, bf16[192,32,128]{2,1,0:T(8,128)(2,1)}) custom-call(s32[4]{0:T(128)} %pad_add_fusion.s_ref, bf16[128,256,256]{2,1,0:T(8,128)(2,1)} %get-tuple-element.240.refs_9_.wre, bf16[128,256,256]{2,1,0:T(8,128)(2,1)} %get-tuple-element.239.refs_10_.wim, ...), custom_call_target="tpu_custom_call" | custom-call | flops 4294967296 | bytes 40000000 | tf_op jit(solution)/shard_map/pallas_call | solution.py:264
  521.9 15.7 %shard_map.76 = (bf16[128,32,128]{2,1,0:T(8,128)(2,1)}, bf16[128,32,128]{2,1,0:T(8,128)(2,1)}, bf16[64,32,128]{2,1,0:T(8,128)(2,1)}, bf16[64,32,128]{2,1,0:T(8,128)(2,1)}) custom-call(s32[4]{0:T(128)} %pad_add_fusion.s_ref, bf16[128,256,256]{2,1,0:T(8,128)(2,1)} %get-tuple-element.240.refs_9_.wre, bf16[128,256,256]{2,1,0:T(8,128)(2,1)} %get-tuple-element.239.refs_10_.wim, ...), custom_call_target="tpu_custom_call" | custom-call | flops 2147483648 | bytes 40000000 | tf_op jit(solution)/shard_map/pallas_call | solution.py:264
  538.5 24.5 %shard_map.82 = (bf16[256,32,128]{2,1,0:T(8,128)(2,1)}, bf16[256,32,128]{2,1,0:T(8,128)(2,1)}, bf16[192,32,128]{2,1,0:T(8,128)(2,1)}, bf16[192,32,128]{2,1,0:T(8,128)(2,1)}) custom-call(s32[4]{0:T(128)} %pad_add_fusion.s_ref, bf16[128,256,256]{2,1,0:T(8,128)(2,1)} %get-tuple-element.240.refs_9_.wre, bf16[128,256,256]{2,1,0:T(8,128)(2,1)} %get-tuple-element.239.refs_10_.wim, ...), custom_call_target="tpu_custom_call" | custom-call | flops 4294967296 | bytes 40000000 | tf_op jit(solution)/shard_map/pallas_call | solution.py:264
  564.3 15.8 %shard_map.81 = (bf16[128,32,128]{2,1,0:T(8,128)(2,1)}, bf16[128,32,128]{2,1,0:T(8,128)(2,1)}, bf16[64,32,128]{2,1,0:T(8,128)(2,1)}, bf16[64,32,128]{2,1,0:T(8,128)(2,1)}) custom-call(s32[4]{0:T(128)} %pad_add_fusion.s_ref, bf16[128,256,256]{2,1,0:T(8,128)(2,1)} %get-tuple-element.240.refs_9_.wre, bf16[128,256,256]{2,1,0:T(8,128)(2,1)} %get-tuple-element.239.refs_10_.wim, ...), custom_call_target="tpu_custom_call" | custom-call | flops 2147483648 | bytes 40000000 | tf_op jit(solution)/shard_map/pallas_call | solution.py:264
  582.0 20.9 %shard_map.78 = (bf16[512,32,256]{2,1,0:T(8,128)(2,1)}, bf16[512,16,256]{2,1,0:T(8,128)(2,1)}, bf16[512,16,256]{2,1,0:T(8,128)(2,1)}) custom-call(s32[4]{0:T(128)} %pad_add_fusion.s_ref, bf16[256,2,128,256]{3,2,1,0:T(8,128)(2,1)} %constant.147.clone.refs_0_.refs_1_.refs_2_.refs_3_, ...), custom_call_target="tpu_custom_call" | custom-call | flops 2791728640 | bytes 50000000 | tf_op jit(solution)/shard_map/pallas_call | solution.py:264
  616.3 20.9 %shard_map.83 = (bf16[512,16,256]{2,1,0:T(8,128)(2,1)}, bf16[512,48,256]{2,1,0:T(8,128)(2,1)}) custom-call(s32[4]{0:T(128)} %pad_add_fusion.s_ref, bf16[256,2,128,256]{3,2,1,0:T(8,128)(2,1)} %constant.147.clone.refs_0_.refs_1_.refs_2_.refs_3_, bf16[256,2,128,256]{3,2,1,0:T(8,128)(2,1)} %constant.147.clone.refs_0_.refs_1_.refs_2_.refs_3_, ...), custom_call_target="tpu_custom_call" | custom-call | flops 2791728640 | bytes 50000000 | tf_op jit(solution)/shard_map/pallas_call | solution.py:264
  652.9 14.7 %shard_map.80 = (bf16[32,64,256]{2,1,0:T(8,128)(2,1)}, bf16[32,64,256]{2,1,0:T(8,128)(2,1)}, bf16[32,64,256]{2,1,0:T(8,128)(2,1)}, bf16[32,64,256]{2,1,0:T(8,128...) custom-call(s32[4]{0:T(128)} %pad_add_fusion.s_ref, ...), custom_call_target="tpu_custom_call" | custom-call | flops 8589934592 | bytes 25165824 | tf_op jit(solution)/shard_map/pallas_call | solution.py:264
  688.1 19.5 %shard_map.84 = (bf16[48,64,256]{2,1,0:T(8,128)(2,1)}, bf16[48,64,256]{2,1,0:T(8,128)(2,1)}, bf16[48,64,256]{2,1,0:T(8,128)(2,1)}, bf16[48,64,256]{2,1,0:T(8,128...) custom-call(s32[4]{0:T(128)} %pad_add_fusion.s_ref, ...), custom_call_target="tpu_custom_call" | custom-call | flops 12884901888 | bytes 37748736 | tf_op jit(solution)/shard_map/pallas_call | solution.py:264
  707.6 32.3 %collective-permute-done.78.refs_7_ = bf16[16,64,256]{2,1,0:T(8,128)(2,1)S(1)} collective-permute-done((bf16[16,64,256]{2,1,0:T(8,128)(2,1)S(1)}, bf16[16,64,256]{2,1,0:T(8,128)(2,1)S(1)}, u32[]{:S(2)}, u32[]{:S(2)}) %collective-permute-start.78) | collective-permute-done | bytes 524320 | tf_op jit(solution)/shard_map/ppermute | solution.py:293
  745.7 22.6 %collective-permute-done.58.refs_5_ = bf16[32,64,256]{2,1,0:T(8,128)(2,1)S(1)} collective-permute-done((bf16[32,64,256]{2,1,0:T(8,128)(2,1)}, bf16[32,64,256]{2,1,0:T(8,128)(2,1)S(1)}, u32[]{:S(2)}, u32[]{:S(2)}) %collective-permute-start.58) | collective-permute-done | bytes 1048608 | tf_op jit(solution)/shard_map/ppermute | solution.py:293
  768.7 32.8 %collective-permute-done.59.refs_6_ = bf16[32,64,256]{2,1,0:T(8,128)(2,1)S(1)} collective-permute-done((bf16[32,64,256]{2,1,0:T(8,128)(2,1)}, bf16[32,64,256]{2,1,0:T(8,128)(2,1)S(1)}, u32[]{:S(2)}, u32[]{:S(2)}) %collective-permute-start.59) | collective-permute-done | bytes 1048608 | tf_op jit(solution)/shard_map/ppermute | solution.py:293
  802.9 19.9 %collective-permute-done.60.refs_7_ = bf16[32,64,256]{2,1,0:T(8,128)(2,1)S(1)} collective-permute-done((bf16[32,64,256]{2,1,0:T(8,128)(2,1)}, bf16[32,64,256]{2,1,0:T(8,128)(2,1)S(1)}, u32[]{:S(2)}, u32[]{:S(2)}) %collective-permute-start.60) | collective-permute-done | bytes 1048608 | tf_op jit(solution)/shard_map/ppermute | solution.py:293
  826.2 30.3 %collective-permute-done.67.refs_3_ = bf16[48,64,256]{2,1,0:T(8,128)(2,1)} collective-permute-done((bf16[48,64,256]{2,1,0:T(8,128)(2,1)}, bf16[48,64,256]{2,1,0:T(8,128)(2,1)}, u32[]{:S(2)}, u32[]{:S(2)}) %collective-permute-start.67) | collective-permute-done | bytes 1572896 | tf_op jit(solution)/shard_map/ppermute | solution.py:293
  859.2 98.6 %collective-permute-done.69.refs_5_ = bf16[48,64,256]{2,1,0:T(8,128)(2,1)} collective-permute-done((bf16[48,64,256]{2,1,0:T(8,128)(2,1)}, bf16[48,64,256]{2,1,0:T(8,128)(2,1)}, u32[]{:S(2)}, u32[]{:S(2)}) %collective-permute-start.69) | collective-permute-done | bytes 1572896 | tf_op jit(solution)/shard_map/ppermute | solution.py:293
  971.9 15.1 %shard_map.86.refs_8_ = f32[4,2,2,64,64,256]{5,4,3,2,1,0:T(8,128)} custom-call(s32[4]{0:T(128)} %pad_add_fusion.s_ref, f32[4,2,2,64,64,256]{5,4,3,2,1,0:T(8,128)} %bitcast.4.refs_0_.refs_1_.refs_2_.refs_3_.refs_4_.refs_5_.refs_6_.refs_7_.f_ref, bf16[16,64,256]{2,1,0:T(8,128)(2,1)} %get-tuple-element.222.refs_0_, ...), custom_call_target="tpu_custom_call" | custom-call | flops 83886080 | bytes 20971520 | tf_op jit(solution)/shard_map/pallas_call | solution.py:264
  987.0 40.8 %shard_map.87.refs_8_ = f32[4,2,2,64,64,256]{5,4,3,2,1,0:T(8,128)} custom-call(s32[4]{0:T(128)} %pad_add_fusion.s_ref, f32[4,2,2,64,64,256]{5,4,3,2,1,0:T(8,128)} %bitcast.4.refs_0_.refs_1_.refs_2_.refs_3_.refs_4_.refs_5_.refs_6_.refs_7_.f_ref, bf16[48,64,256]{2,1,0:T(8,128)(2,1)} %get-tuple-element.213.refs_0_, ...), custom_call_target="tpu_custom_call", output_to_operand_aliasing={{}: (10, {})} | custom-call | flops 251658240 | bytes 62914560 | tf_op jit(solution)/shard_map/pallas_call | solution.py:264
  1027.8 28.1 %shard_map.88.refs_8_ = f32[4,2,2,64,64,256]{5,4,3,2,1,0:T(8,128)} custom-call(s32[4]{0:T(128)} %pad_add_fusion.s_ref, f32[4,2,2,64,64,256]{5,4,3,2,1,0:T(8,128)} %bitcast.4.refs_0_.refs_1_.refs_2_.refs_3_.refs_4_.refs_5_.refs_6_.refs_7_.f_ref, bf16[32,64,256]{2,1,0:T(8,128)(2,1)} %get-tuple-element.196.refs_0_, ...), custom_call_target="tpu_custom_call", output_to_operand_aliasing={{}: (10, {})} | custom-call | flops 167772160 | bytes 41943040 | tf_op jit(solution)/shard_map/pallas_call | solution.py:264
  1059.5 15.2 %shard_map.89 = f32[4,2,2,64,64,256]{5,4,3,2,1,0:T(8,128)} custom-call(s32[4]{0:T(128)} %pad_add_fusion.s_ref, f32[4,2,2,64,64,256]{5,4,3,2,1,0:T(8,128)} %bitcast.4.refs_0_.refs_1_.refs_2_.refs_3_.refs_4_.refs_5_.refs_6_.refs_7_.f_ref, bf16[16,64,256]{2,1,0:T(8,128)(2,1)} %get-tuple-element.187.refs_0_, ...), custom_call_target="tpu_custom_call", output_to_operand_aliasing={{}: (10, {})} | custom-call | flops 83886080 | bytes 20971520 | tf_op jit(solution)/shard_map/pallas_call | solution.py:264
  1089.4 16.0 %collective-permute-done.83 = bf16[16,64,256]{2,1,0:T(8,128)(2,1)S(1)} collective-permute-done((bf16[16,64,256]{2,1,0:T(8,128)(2,1)S(1)}, bf16[16,64,256]{2,1,0:T(8,128)(2,1)S(1)}, u32[]{:S(2)}, u32[]{:S(2)}) %collective-permute-start.83) | collective-permute-done | bytes 524320 | tf_op jit(solution)/shard_map/ppermute | solution.py:293
  (271 shorter events, 277.2 us)
Async XLA Ops:
  103.2 82.3 %collective-permute-start.7 = (bf16[48,64,256]{2,1,0:T(8,128)(2,1)}, bf16[48,64,256]{2,1,0:T(8,128)(2,1)S(1)}, u32[]{:S(2)}, u32[]{:S(2)}) collective-permute-start(bf16[48,64,256]{2,1,0:T(8,128)(2,1)} %get-tuple-element.131), channel_id=1, source_target_pairs={{0,1},{1,0},{2,3},{3,2},{4,5},{5,4},{6,7},{7,6}} | collective-permute-start | bytes 4718600 | tf_op jit(solution)/shard_map/ppermute | solution.py:293
  112.2 75.4 %collective-permute-start.8 = (bf16[48,64,256]{2,1,0:T(8,128)(2,1)}, bf16[48,64,256]{2,1,0:T(8,128)(2,1)S(1)}, u32[]{:S(2)}, u32[]{:S(2)}) collective-permute-start(bf16[48,64,256]{2,1,0:T(8,128)(2,1)} %get-tuple-element.132), channel_id=1, source_target_pairs={{0,2},{1,3},{2,0},{3,1},{4,6},{5,7},{6,4},{7,5}} | collective-permute-start | bytes 4718600 | tf_op jit(solution)/shard_map/ppermute | solution.py:293
  113.0 70.4 %collective-permute-start.14 = (bf16[32,64,256]{2,1,0:T(8,128)(2,1)}, bf16[32,64,256]{2,1,0:T(8,128)(2,1)}, u32[]{:S(2)}, u32[]{:S(2)}) collective-permute-start(bf16[32,64,256]{2,1,0:T(8,128)(2,1)} %get-tuple-element.140), channel_id=1, source_target_pairs={{0,1},{1,0},{2,3},{3,2},{4,5},{5,4},{6,7},{7,6}} | collective-permute-start | bytes 3145736 | tf_op jit(solution)/shard_map/ppermute | solution.py:293
  113.4 71.8 %collective-permute-start.15 = (bf16[32,64,256]{2,1,0:T(8,128)(2,1)}, bf16[32,64,256]{2,1,0:T(8,128)(2,1)}, u32[]{:S(2)}, u32[]{:S(2)}) collective-permute-start(bf16[32,64,256]{2,1,0:T(8,128)(2,1)} %get-tuple-element.141), channel_id=1, source_target_pairs={{0,2},{1,3},{2,0},{3,1},{4,6},{5,7},{6,4},{7,5}} | collective-permute-start | bytes 3145736 | tf_op jit(solution)/shard_map/ppermute | solution.py:293
  114.6 68.6 %collective-permute-start.29 = (bf16[16,64,256]{2,1,0:T(8,128)(2,1)}, bf16[16,64,256]{2,1,0:T(8,128)(2,1)}, u32[]{:S(2)}, u32[]{:S(2)}) collective-permute-start(bf16[16,64,256]{2,1,0:T(8,128)(2,1)} %get-tuple-element.158), channel_id=1, source_target_pairs={{0,2},{1,3},{2,0},{3,1},{4,6},{5,7},{6,4},{7,5}} | collective-permute-start | bytes 1572872 | tf_op jit(solution)/shard_map/ppermute | solution.py:293
  183.4 104.3 %collective-permute-start.10 = (bf16[48,64,256]{2,1,0:T(8,128)(2,1)}, bf16[48,64,256]{2,1,0:T(8,128)(2,1)}, u32[]{:S(2)}, u32[]{:S(2)}) collective-permute-start(bf16[48,64,256]{2,1,0:T(8,128)(2,1)} %get-tuple-element.134), channel_id=1, source_target_pairs={{0,4},{1,5},{2,6},{3,7},{4,0},{5,1},{6,2},{7,3}} | collective-permute-start | bytes 4718600 | tf_op jit(solution)/shard_map/ppermute | solution.py:293
  185.2 136.4 %collective-permute-start.11 = (bf16[48,64,256]{2,1,0:T(8,128)(2,1)}, bf16[48,64,256]{2,1,0:T(8,128)(2,1)}, u32[]{:S(2)}, u32[]{:S(2)}) collective-permute-start(bf16[48,64,256]{2,1,0:T(8,128)(2,1)} %get-tuple-element.135), channel_id=1, source_target_pairs={{0,5},{1,4},{2,7},{3,6},{4,1},{5,0},{6,3},{7,2}} | collective-permute-start | bytes 4718600 | tf_op jit(solution)/shard_map/ppermute | solution.py:293
  185.5 137.9 %collective-permute-start.12 = (bf16[48,64,256]{2,1,0:T(8,128)(2,1)}, bf16[48,64,256]{2,1,0:T(8,128)(2,1)}, u32[]{:S(2)}, u32[]{:S(2)}) collective-permute-start(bf16[48,64,256]{2,1,0:T(8,128)(2,1)} %get-tuple-element.136), channel_id=1, source_target_pairs={{0,6},{1,7},{2,4},{3,5},{4,2},{5,3},{6,0},{7,1}} | collective-permute-start | bytes 4718600 | tf_op jit(solution)/shard_map/ppermute | solution.py:293
  187.6 136.4 %collective-permute-start.13 = (bf16[48,64,256]{2,1,0:T(8,128)(2,1)}, bf16[48,64,256]{2,1,0:T(8,128)(2,1)}, u32[]{:S(2)}, u32[]{:S(2)}) collective-permute-start(bf16[48,64,256]{2,1,0:T(8,128)(2,1)} %get-tuple-element.137), channel_id=1, source_target_pairs={{0,7},{1,6},{2,5},{3,4},{4,3},{5,2},{6,1},{7,0}} | collective-permute-start | bytes 4718600 | tf_op jit(solution)/shard_map/ppermute | solution.py:293
  221.4 144.8 %collective-permute-start.16 = (bf16[32,64,256]{2,1,0:T(8,128)(2,1)}, bf16[32,64,256]{2,1,0:T(8,128)(2,1)}, u32[]{:S(2)}, u32[]{:S(2)}) collective-permute-start(bf16[32,64,256]{2,1,0:T(8,128)(2,1)} %get-tuple-element.142), channel_id=1, source_target_pairs={{0,3},{1,2},{2,1},{3,0},{4,7},{5,6},{6,5},{7,4}} | collective-permute-start | bytes 3145736 | tf_op jit(solution)/shard_map/ppermute | solution.py:293
  287.7 101.8 %collective-permute-start.17 = (bf16[32,64,256]{2,1,0:T(8,128)(2,1)S(1)}, bf16[32,64,256]{2,1,0:T(8,128)(2,1)}, u32[]{:S(2)}, u32[]{:S(2)}) collective-permute-start(bf16[32,64,256]{2,1,0:T(8,128)(2,1)S(1)} %copy-done.32), channel_id=1, source_target_pairs={{0,4},{1,5},{2,6},{3,7},{4,0},{5,1},{6,2},{7,3}} | collective-permute-start | bytes 3145736 | tf_op jit(solution)/shard_map/ppermute | solution.py:293
  321.6 89.9 %collective-permute-start.18 = (bf16[32,64,256]{2,1,0:T(8,128)(2,1)S(1)}, bf16[32,64,256]{2,1,0:T(8,128)(2,1)}, u32[]{:S(2)}, u32[]{:S(2)}) collective-permute-start(bf16[32,64,256]{2,1,0:T(8,128)(2,1)S(1)} %copy-done.31), channel_id=1, source_target_pairs={{0,5},{1,4},{2,7},{3,6},{4,1},{5,0},{6,3},{7,2}} | collective-permute-start | bytes 3145736 | tf_op jit(solution)/shard_map/ppermute | solution.py:293
  323.3 89.9 %collective-permute-start.19 = (bf16[32,64,256]{2,1,0:T(8,128)(2,1)S(1)}, bf16[32,64,256]{2,1,0:T(8,128)(2,1)}, u32[]{:S(2)}, u32[]{:S(2)}) collective-permute-start(bf16[32,64,256]{2,1,0:T(8,128)(2,1)S(1)} %copy-done.30), channel_id=1, source_target_pairs={{0,6},{1,7},{2,4},{3,5},{4,2},{5,3},{6,0},{7,1}} | collective-permute-start | bytes 3145736 | tf_op jit(solution)/shard_map/ppermute | solution.py:293
  324.1 89.9 %collective-permute-start.20 = (bf16[32,64,256]{2,1,0:T(8,128)(2,1)S(1)}, bf16[32,64,256]{2,1,0:T(8,128)(2,1)}, u32[]{:S(2)}, u32[]{:S(2)}) collective-permute-start(bf16[32,64,256]{2,1,0:T(8,128)(2,1)S(1)} %copy-done.29), channel_id=1, source_target_pairs={{0,7},{1,6},{2,5},{3,4},{4,3},{5,2},{6,1},{7,0}} | collective-permute-start | bytes 3145736 | tf_op jit(solution)/shard_map/ppermute | solution.py:293
  366.3 73.4 %collective-permute-start.30 = (bf16[16,64,256]{2,1,0:T(8,128)(2,1)S(1)}, bf16[16,64,256]{2,1,0:T(8,128)(2,1)S(1)}, u32[]{:S(2)}, u32[]{:S(2)}) collective-permute-start(bf16[16,64,256]{2,1,0:T(8,128)(2,1)S(1)} %copy-done.39), channel_id=1, source_target_pairs={{0,3},{1,2},{2,1},{3,0},{4,7},{5,6},{6,5},{7,4}} | collective-permute-start | bytes 1572872 | tf_op jit(solution)/shard_map/ppermute | solution.py:293
  521.7 58.9 %collective-permute-start.46 = (bf16[256,32,128]{2,1,0:T(8,128)(2,1)}, bf16[256,32,128]{2,1,0:T(8,128)(2,1)S(1)}, u32[]{:S(2)}, u32[]{:S(2)}) collective-permute-start(bf16[256,32,128]{2,1,0:T(8,128)(2,1)} %get-tuple-element.185), channel_id=1, source_target_pairs={{0,1},{1,0},{2,3},{3,2},{4,5},{5,4},{6,7},{7,6}} | collective-permute-start | bytes 6291464 | tf_op jit(solution)/shard_map/ppermute | solution.py:293
  667.6 73.9 %collective-permute-start.54 = (bf16[32,64,256]{2,1,0:T(8,128)(2,1)}, bf16[32,64,256]{2,1,0:T(8,128)(2,1)S(1)}, u32[]{:S(2)}, u32[]{:S(2)}) collective-permute-start(bf16[32,64,256]{2,1,0:T(8,128)(2,1)} %get-tuple-element.197), channel_id=1, source_target_pairs={{0,1},{1,0},{2,3},{3,2},{4,5},{5,4},{6,7},{7,6}} | collective-permute-start | bytes 3145736 | tf_op jit(solution)/shard_map/ppermute | solution.py:293
  672.3 70.4 %collective-permute-start.55 = (bf16[32,64,256]{2,1,0:T(8,128)(2,1)}, bf16[32,64,256]{2,1,0:T(8,128)(2,1)S(1)}, u32[]{:S(2)}, u32[]{:S(2)}) collective-permute-start(bf16[32,64,256]{2,1,0:T(8,128)(2,1)} %get-tuple-element.198), channel_id=1, source_target_pairs={{0,2},{1,3},{2,0},{3,1},{4,6},{5,7},{6,4},{7,5}} | collective-permute-start | bytes 3145736 | tf_op jit(solution)/shard_map/ppermute | solution.py:293
  673.1 69.6 %collective-permute-start.56 = (bf16[32,64,256]{2,1,0:T(8,128)(2,1)}, bf16[32,64,256]{2,1,0:T(8,128)(2,1)}, u32[]{:S(2)}, u32[]{:S(2)}) collective-permute-start(bf16[32,64,256]{2,1,0:T(8,128)(2,1)} %get-tuple-element.199), channel_id=1, source_target_pairs={{0,3},{1,2},{2,1},{3,0},{4,7},{5,6},{6,5},{7,4}} | collective-permute-start | bytes 3145736 | tf_op jit(solution)/shard_map/ppermute | solution.py:293
  740.7 84.2 %collective-permute-start.65 = (bf16[48,64,256]{2,1,0:T(8,128)(2,1)}, bf16[48,64,256]{2,1,0:T(8,128)(2,1)S(1)}, u32[]{:S(2)}, u32[]{:S(2)}) collective-permute-start(bf16[48,64,256]{2,1,0:T(8,128)(2,1)} %get-tuple-element.214), channel_id=1, source_target_pairs={{0,1},{1,0},{2,3},{3,2},{4,5},{5,4},{6,7},{7,6}} | collective-permute-start | bytes 4718600 | tf_op jit(solution)/shard_map/ppermute | solution.py:293
  741.5 84.7 %collective-permute-start.66 = (bf16[48,64,256]{2,1,0:T(8,128)(2,1)}, bf16[48,64,256]{2,1,0:T(8,128)(2,1)S(1)}, u32[]{:S(2)}, u32[]{:S(2)}) collective-permute-start(bf16[48,64,256]{2,1,0:T(8,128)(2,1)} %get-tuple-element.215), channel_id=1, source_target_pairs={{0,2},{1,3},{2,0},{3,1},{4,6},{5,7},{6,4},{7,5}} | collective-permute-start | bytes 4718600 | tf_op jit(solution)/shard_map/ppermute | solution.py:293
  742.7 58.8 %collective-permute-start.59 = (bf16[32,64,256]{2,1,0:T(8,128)(2,1)}, bf16[32,64,256]{2,1,0:T(8,128)(2,1)S(1)}, u32[]{:S(2)}, u32[]{:S(2)}) collective-permute-start(bf16[32,64,256]{2,1,0:T(8,128)(2,1)} %get-tuple-element.202), channel_id=1, source_target_pairs={{0,6},{1,7},{2,4},{3,5},{4,2},{5,3},{6,0},{7,1}} | collective-permute-start | bytes 3145736 | tf_op jit(solution)/shard_map/ppermute | solution.py:293
  744.3 78.5 %collective-permute-start.60 = (bf16[32,64,256]{2,1,0:T(8,128)(2,1)}, bf16[32,64,256]{2,1,0:T(8,128)(2,1)S(1)}, u32[]{:S(2)}, u32[]{:S(2)}) collective-permute-start(bf16[32,64,256]{2,1,0:T(8,128)(2,1)} %get-tuple-element.203), channel_id=1, source_target_pairs={{0,7},{1,6},{2,5},{3,4},{4,3},{5,2},{6,1},{7,0}} | collective-permute-start | bytes 3145736 | tf_op jit(solution)/shard_map/ppermute | solution.py:293
  768.3 88.2 %collective-permute-start.67 = (bf16[48,64,256]{2,1,0:T(8,128)(2,1)}, bf16[48,64,256]{2,1,0:T(8,128)(2,1)}, u32[]{:S(2)}, u32[]{:S(2)}) collective-permute-start(bf16[48,64,256]{2,1,0:T(8,128)(2,1)} %get-tuple-element.216), channel_id=1, source_target_pairs={{0,3},{1,2},{2,1},{3,0},{4,7},{5,6},{6,5},{7,4}} | collective-permute-start | bytes 4718600 | tf_op jit(solution)/shard_map/ppermute | solution.py:293
  822.8 135.0 %collective-permute-start.69 = (bf16[48,64,256]{2,1,0:T(8,128)(2,1)}, bf16[48,64,256]{2,1,0:T(8,128)(2,1)}, u32[]{:S(2)}, u32[]{:S(2)}) collective-permute-start(bf16[48,64,256]{2,1,0:T(8,128)(2,1)} %get-tuple-element.218), channel_id=1, source_target_pairs={{0,5},{1,4},{2,7},{3,6},{4,1},{5,0},{6,3},{7,2}} | collective-permute-start | bytes 4718600 | tf_op jit(solution)/shard_map/ppermute | solution.py:293
  824.8 135.1 %collective-permute-start.70 = (bf16[48,64,256]{2,1,0:T(8,128)(2,1)}, bf16[48,64,256]{2,1,0:T(8,128)(2,1)}, u32[]{:S(2)}, u32[]{:S(2)}) collective-permute-start(bf16[48,64,256]{2,1,0:T(8,128)(2,1)} %get-tuple-element.219), channel_id=1, source_target_pairs={{0,6},{1,7},{2,4},{3,5},{4,2},{5,3},{6,0},{7,1}} | collective-permute-start | bytes 4718600 | tf_op jit(solution)/shard_map/ppermute | solution.py:293
  826.2 143.9 %collective-permute-start.71 = (bf16[48,64,256]{2,1,0:T(8,128)(2,1)}, bf16[48,64,256]{2,1,0:T(8,128)(2,1)S(1)}, u32[]{:S(2)}, u32[]{:S(2)}) collective-permute-start(bf16[48,64,256]{2,1,0:T(8,128)(2,1)} %get-tuple-element.220), channel_id=1, source_target_pairs={{0,7},{1,6},{2,5},{3,4},{4,3},{5,2},{6,1},{7,0}} | collective-permute-start | bytes 4718600 | tf_op jit(solution)/shard_map/ppermute | solution.py:293
  856.5 199.4 %collective-permute-start.50 = (bf16[16,64,256]{2,1,0:T(8,128)(2,1)}, bf16[16,64,256]{2,1,0:T(8,128)(2,1)}, u32[]{:S(2)}, u32[]{:S(2)}) collective-permute-start(bf16[16,64,256]{2,1,0:T(8,128)(2,1)} %get-tuple-element.191), channel_id=1, source_target_pairs={{0,4},{1,5},{2,6},{3,7},{4,0},{5,1},{6,2},{7,3}} | collective-permute-start | bytes 1572872 | tf_op jit(solution)/shard_map/ppermute | solution.py:293
  857.9 199.3 %collective-permute-start.51 = (bf16[16,64,256]{2,1,0:T(8,128)(2,1)}, bf16[16,64,256]{2,1,0:T(8,128)(2,1)}, u32[]{:S(2)}, u32[]{:S(2)}) collective-permute-start(bf16[16,64,256]{2,1,0:T(8,128)(2,1)} %get-tuple-element.192), channel_id=1, source_target_pairs={{0,5},{1,4},{2,7},{3,6},{4,1},{5,0},{6,3},{7,2}} | collective-permute-start | bytes 1572872 | tf_op jit(solution)/shard_map/ppermute | solution.py:293
  957.9 99.5 %collective-permute-start.52 = (bf16[16,64,256]{2,1,0:T(8,128)(2,1)}, bf16[16,64,256]{2,1,0:T(8,128)(2,1)}, u32[]{:S(2)}, u32[]{:S(2)}) collective-permute-start(bf16[16,64,256]{2,1,0:T(8,128)(2,1)} %get-tuple-element.193), channel_id=1, source_target_pairs={{0,6},{1,7},{2,4},{3,5},{4,2},{5,3},{6,0},{7,1}} | collective-permute-start | bytes 1572872 | tf_op jit(solution)/shard_map/ppermute | solution.py:293
  959.9 98.7 %collective-permute-start.53 = (bf16[16,64,256]{2,1,0:T(8,128)(2,1)}, bf16[16,64,256]{2,1,0:T(8,128)(2,1)}, u32[]{:S(2)}, u32[]{:S(2)}) collective-permute-start(bf16[16,64,256]{2,1,0:T(8,128)(2,1)} %get-tuple-element.194), channel_id=1, source_target_pairs={{0,7},{1,6},{2,5},{3,4},{4,3},{5,2},{6,1},{7,0}} | collective-permute-start | bytes 1572872 | tf_op jit(solution)/shard_map/ppermute | solution.py:293
  971.2 106.0 %collective-permute-start.79 = (bf16[16,64,256]{2,1,0:T(8,128)(2,1)}, bf16[16,64,256]{2,1,0:T(8,128)(2,1)}, u32[]{:S(2)}, u32[]{:S(2)}) collective-permute-start(bf16[16,64,256]{2,1,0:T(8,128)(2,1)} %get-tuple-element.232), channel_id=1, source_target_pairs={{0,1},{1,0},{2,3},{3,2},{4,5},{5,4},{6,7},{7,6}} | collective-permute-start | bytes 1572872 | tf_op jit(solution)/shard_map/ppermute | solution.py:293
  (100 other events, 3426.2 us)

commit v2 on v1

--- a/solution.py
+++ b/solution.py
@@ -45,7 +45,8 @@
 
     def pack(p):
         p = p.astype(np.float32).astype(BF).reshape(n_deg, n_deg // (2 * LB), 2, LB, n_lat)
-        return np.ascontiguousarray(p.transpose(0, 2, 1, 3, 4)).reshape(n_deg, 2, n_deg // 2, n_lat)
+        p = p.transpose(0, 2, 1, 3, 4).reshape(n_deg, 2, NV, n_deg // 2 // NV, n_lat)
+        return [np.ascontiguousarray(p[:MG * (v + 1), :, v]) for v in range(NV)]
 
     return pack(tab * (w / n_lon)), pack(tab)
 
@@ -116,8 +117,11 @@
                     p = jnp.concatenate([pws[v][m, h] for v in range(g, NV)] + [pws[v][m, 1 - h] for v in range(g, NV)], axis=0)
                     res = lax.dot_general(p, x, NT, preferred_element_type=F32).astype(BF)
                     for v in range(g, NV):
-                        mine[v][m] = res[(v - g) * nl:(v - g + 1) * nl]
-                        send[v][m] = res[(NV + v - 2 * g) * nl:(NV + v - 2 * g + 1) * nl]
+                        for b in range(nl // LB):
+                            at = (v - g) * nl + b * LB
+                            mine[v][b, m] = res[at:at + LB]
+                            at += (NV - g) * nl
+                            send[v][b, m] = res[at:at + LB]
                 return carry
 
             lax.fori_loop(0, MB // 8, body, 0)
@@ -137,8 +141,8 @@
                 for u in range(16):
                     rows = pl.ds((i * 16 + u) * PAD, LB)
                     for half in range(2):
-                        scr_a[2 * half + h, rows, :] = ins[v][half][i * 16 + u].astype(F32)
-                        scr_a[2 * half + 1 - h, rows, :] = ins[v][2 + half][i * 16 + u].astype(F32)
+                        scr_a[2 * half + h, rows, :] = ins[v][half][0, i * 16 + u].astype(F32)
+                        scr_a[2 * half + 1 - h, rows, :] = ins[v][2 + half][0, i * 16 + u].astype(F32)
                 return carry
 
             lax.fori_loop(0, nm // 16, fill, 0)
@@ -167,8 +171,8 @@
                     re, im = scr_b[0, rows, :], scr_b[1, rows, :]
                     zero = jnp.where(low, re, pltpu.roll(im, 64, 1))
                     one = jnp.where(low, pltpu.roll(re, 64, 1), im)
-                    outs[v][0][i * 16 + u] = jnp.where(first_is_mine, zero, one).astype(BF)
-                    outs[v][1][i * 16 + u] = jnp.where(first_is_mine, one, zero).astype(BF)
+                    outs[v][0][0, i * 16 + u] = jnp.where(first_is_mine, zero, one).astype(BF)
+                    outs[v][1][0, i * 16 + u] = jnp.where(first_is_mine, one, zero).astype(BF)
                 return carry
 
             lax.fori_loop(0, nm // 16, flush, 0)
@@ -185,7 +189,7 @@
             def body(m8, carry):
                 for u in range(8):
                     m = m8 * 8 + u
-                    b = jnp.concatenate([bm[v][m] for v in range(g, NV)] + [br[v][m] for v in range(g, NV)], axis=0)
+                    b = jnp.concatenate([x[v][lb, m] for x in (bm, br) for v in range(g, NV) for lb in range(2)], axis=0)
                     p = jnp.concatenate([pis[v][m, h] for v in range(g, NV)] + [pis[v][m, 1 - h] for v in range(g, NV)], axis=0)
                     y = lax.dot_general(b, p, TN, preferred_element_type=F32).astype(BF)
                     off = 0
@@ -284,7 +288,8 @@
         scal = jnp.stack([me, q, r, h]).astype(jnp.int32)
         pw_np, pi_np = legendre_tables(n_lat, n_lon, n_deg)
         tf_np, ti_np = dft_tables(n_lon, n_deg)
-        pw, pi, tf, ti = jnp.asarray(pw_np), jnp.asarray(pi_np), jnp.asarray(tf_np), jnp.asarray(ti_np)
+        pw, pi = [jnp.asarray(x) for x in pw_np], [jnp.asarray(x) for x in pi_np]
+        tf, ti = jnp.asarray(tf_np), jnp.asarray(ti_np)
         f6 = grid_field.reshape(batch, 2, channels // half_c, half_c // 2, row_count, col_count)
 
         def swap(x, t):
@@ -318,9 +323,9 @@
                 4.0 * cc * nms * n_lat * n_lon, cc * nms * n_lat * 6, dft_scratch, deps)(scal, tf, *pieces)
 
         last = [MG // MB * (v + 1) - 1 for v in range(NV)]
-        tri_specs = [pl.BlockSpec((MB, 2, lv, n_lat), functools.partial(lambda v, i, s: (jnp.minimum(i, last[v]), 0, v, 0), v)) for v in range(NV)]
-        spec_specs = [pl.BlockSpec((MB, lv, half_c), functools.partial(lambda v, i, s: (jnp.minimum(i, last[v]), 0, 0), v)) for v in range(NV)]
-        spec_shapes = [jax.ShapeDtypeStruct((MG * (v + 1), lv, half_c), BF) for v in range(NV)]
+        tri_specs = [pl.BlockSpec((MB, 2, lv, n_lat), functools.partial(lambda v, i, s: (jnp.minimum(i, last[v]), 0, 0, 0), v)) for v in range(NV)]
+        spec_specs = [pl.BlockSpec((lv // LB, MB, LB, half_c), functools.partial(lambda v, i, s: (0, jnp.minimum(i, last[v]), 0, 0), v)) for v in range(NV)]
+        spec_shapes = [jax.ShapeDtypeStruct((lv // LB, MG * (v + 1), LB, half_c), BF) for v in range(NV)]
 
         def f_spec(cc):
             return pl.BlockSpec((2 * MB, cc, n_lat), lambda i, s: (i, 0, 0))
@@ -330,7 +335,7 @@
                 functools.partial(fwd_leg_kernel, len(fs)), (n_deg // MB,),
                 tri_specs + [f_spec(f.shape[1]) for f in fs],
                 spec_specs * 2, spec_shapes * 2,
-                1.3 * n_deg * n_deg * n_lat * half_c, 50e6)(scal, *([pw] * NV), *fs)
+                1.3 * n_deg * n_deg * n_lat * half_c, 50e6)(scal, *pw, *fs)
             return res[:NV], res[NV:]
 
         def leg_inv(half, mine, recv, deps=()):
@@ -339,7 +344,7 @@
                 tri_specs + spec_specs * 2,
                 [f_spec(cc) for cc in HALVES[half]],
                 [jax.ShapeDtypeStruct((nms, cc, n_lat), BF) for cc in HALVES[half]],
-                1.3 * n_deg * n_deg * n_lat * half_c, 50e6, (), deps)(scal, *([pi] * NV), *mine, *recv)
+                1.3 * n_deg * n_deg * n_lat * half_c, 50e6, (), deps)(scal, *pi, *mine, *recv)
 
         sizes = HALVES[0] + HALVES[1]
         starts = [(half, sum(part[:k])) for half, part in enumerate(HALVES) for k in range(len(part))]
@@ -351,7 +356,8 @@
 
         w = mix_weight.reshape(n_deg // (2 * LB), 2, LB, channels, channels, 2)
         w = lax.dynamic_index_in_dim(w, h, axis=1, keepdims=False).reshape(n_deg // 2, channels, channels, 2)
-        w_re, w_im = w[..., 0], w[..., 1]
+        oh = channels // 2
+        w_parts = [[w[:, :, x * oh:(x + 1) * oh, p] for p in range(2)] for x in range(2)]
 
         a_mine, a_recv, prev = [], [], []
         k = 0
@@ -360,7 +366,7 @@
             for cc in HALVES[half]:
                 deps = list(prev)
                 if k == 1:
-                    deps += [w_re, w_im]
+                    deps += w_parts[0] + w_parts[1]
                 elif k == len(HALVES[0]):
                     deps += [a_mine[0][0]]
                 fs.append(dft_chunk(recv[k], cc, deps))
@@ -376,10 +382,10 @@
         def mix(vs, out_half):
             first = vs[0] * 2
             jump = [lambda j: jnp.minimum(j, 1), lambda j: jnp.maximum(j - 2, 0)]
-            w_spec = pl.BlockSpec((LB, channels, channels // 2), lambda j, s: (jnp.where(j < 2, first + j, first + j - 4), 0, out_half))
+            w_spec = pl.BlockSpec((LB, channels, channels // 2), lambda j, s: (jnp.where(j < 2, first + j, first + j - 4), 0, 0))
             specs, outs, shapes, args = [], [], [], []
             for n, v in enumerate(vs):
-                spec = pl.BlockSpec((MG * (v + 1), LB, half_c), functools.partial(lambda n, j, s: (0, jump[n](j), 0), n))
+                spec = pl.BlockSpec((1, MG * (v + 1), LB, half_c), functools.partial(lambda n, j, s: (jump[n](j), 0, 0, 0), n))
                 specs += [spec] * 4
                 outs += [spec] * 2
                 shapes += [spec_shapes[v]] * 2
@@ -388,7 +394,7 @@
             return call(
                 functools.partial(mix_kernel, vs), (4,), [w_spec, w_spec] + specs, outs, shapes,
                 4.0 * 4 * LB * MG * (vs[0] + 1) * channels * channels, 40e6,
-                [pltpu.VMEM((4, rows, 128), F32), pltpu.VMEM((2, rows, 128), F32)])(scal, w_re, w_im, *args)
+                [pltpu.VMEM((4, rows, 128), F32), pltpu.VMEM((2, rows, 128), F32)])(scal, *w_parts[out_half], *args)
 
         def mix_half(half):
             mine, recv = [None] * NV, [None] * NV

time: 1120 us -> 1110 us (level)
  no operation moved by 1% of the time
where the time goes in v2:
time: 1110 us
  waiting for transfers between devices  494 us (45%)
  Pallas kernels  432 us (39%)
  local copies, waits for them, and re-layouts  84.4 us (8%)
  starting transfers between devices  80.7 us (7%)
  other arithmetic  20.4 us (2%)
    ppermute x86, waiting for transfers between devices, swap(): return lax.ppermute(x, ('lon', 'lat'), [(s, s ^ t) for s in range(nd)])  494 us
    pallas_call x27, Pallas kernels, call(): return lambda *args: fn(*args, *deps)  432 us
    ppermute x86, starting transfers between devices, swap(): return lax.ppermute(x, ('lon', 'lat'), [(s, s ^ t) for s in range(nd)])  80.7 us
    unnamed x93, local copies, waits for them, and re-layouts  34.3 us
    dynamic_slice x1, local copies, waits for them, and re-layouts, local_layer(): lax.dynamic_index_in_dim(w, h, axis=1, keepdims=False)  26.7 us
    squeeze x1, local copies, waits for them, and re-layouts, local_layer(): w[:, :, x * oh:(x + 1) * oh, p]  23.4 us
  transfers between devices with their start and end apart: 86, of which 24 were waited for; matrix products, arithmetic and copies ran while one was open for 8% of the time, Pallas kernels for 38%

profile of v2, /device:TPU:0, one launch (start us, length us, event | category | flops | bytes accessed | tf_op | source)
XLA Modules:
  0.0 1111.3 jit_solution(6223772023985572136)
XLA Ops:
  36.4 21.1 %collective-permute-done.4.refs_5_ = bf16[16,64,256]{2,1,0:T(8,128)(2,1)} collective-permute-done((bf16[16,64,256]{2,1,0:T(8,128)(2,1)}, bf16[16,64,256]{2,1,0:T(8,128)(2,1)}, u32[]{:S(2)}, u32[]{:S(2)}) %collective-permute-start.4) | collective-permute-done | bytes 524320 | tf_op jit(solution)/shard_map/ppermute | solution.py:298
  115.4 26.7 %constant_dynamic-slice_fusion = bf16[8,1,16,256,256,2]{4,5,3,2,1,0:T(2,128)(2,1)} fusion(bf16[8,2,16,256,256,2]{4,5,3,2,1,0:T(2,128)(2,1)} %bitcast.5, s32[]{:T(128)S(6)} %select_n.133), kind=kLoop, calls=%fused_computation.68 | loop fusion | bytes 67108864 | tf_op jit(solution)/shard_map/jit(dynamic_index_in_dim)/dynamic_slice | solution.py:358
  142.1 22.7 %copy.17 = bf16[8,1,16,256,256,2]{4,3,2,0,5,1:T(8,128)(2,1)} copy(bf16[8,1,16,256,256,2]{4,5,3,2,1,0:T(2,128)(2,1)} %constant_dynamic-slice_fusion) | data formatting | bytes 67108864
  164.8 18.3 %collective-permute-done.29.refs_2_ = bf16[16,64,256]{2,1,0:T(8,128)(2,1)} collective-permute-done((bf16[16,64,256]{2,1,0:T(8,128)(2,1)}, bf16[16,64,256]{2,1,0:T(8,128)(2,1)}, u32[]{:S(2)}, u32[]{:S(2)}) %collective-permute-start.29) | collective-permute-done | bytes 524320 | tf_op jit(solution)/shard_map/ppermute | solution.py:298
  187.8 23.4 %slice_bitcast_fusion = (bf16[128,256,128]{2,1,0:T(8,128)(2,1)}, bf16[128,256,128]{2,1,0:T(8,128)(2,1)}, bf16[128,256,128]{2,1,0:T(8,128)(2,1)}, bf16[128,256,128]{2,1,0:T(8,128)(2,1)}) fusion(bf16[128,256,256,2]{2,1,0,3:T(8,128)(2,1)} %bitcast.64), kind=kLoop, calls=%fused_computation | loop fusion | bytes 67108864 | tf_op jit(solution)/shard_map/squeeze | solution.py:360
  222.5 65.1 %collective-permute-done.10.refs_4_ = bf16[48,64,256]{2,1,0:T(8,128)(2,1)} collective-permute-done((bf16[48,64,256]{2,1,0:T(8,128)(2,1)}, bf16[48,64,256]{2,1,0:T(8,128)(2,1)}, u32[]{:S(2)}, u32[]{:S(2)}) %collective-permute-start.10) | collective-permute-done | bytes 1572896 | tf_op jit(solution)/shard_map/ppermute | solution.py:298
  290.2 31.4 %collective-permute-done.11.refs_5_ = bf16[48,64,256]{2,1,0:T(8,128)(2,1)} collective-permute-done((bf16[48,64,256]{2,1,0:T(8,128)(2,1)}, bf16[48,64,256]{2,1,0:T(8,128)(2,1)}, u32[]{:S(2)}, u32[]{:S(2)}) %collective-permute-start.11) | collective-permute-done | bytes 1572896 | tf_op jit(solution)/shard_map/ppermute | solution.py:298
  325.2 19.6 %shard_map.121.refs_5_.refs_8_ = bf16[512,48,256]{2,1,0:T(8,128)(2,1)} custom-call(s32[4]{0:T(128)} %pad_add_fusion.s_ref, bf16[2,512,512]{2,1,0:T(8,128)(2,1)} %constant.166.clone.tab_ref, bf16[48,64,256]{2,1,0:T(8,128)(2,1)} %get-tuple-element.130.refs_0_, bf16[48,64,256]{2,1,0:T(8,128)(2,1)} %copy-done.10, bf16[48,64,256]{2,1,0:T(8,128)(2,1)} %copy-done.11, ...), custom_call_target="tpu_custom_call" | custom-call | flops 12884901888 | bytes 37748736 | tf_op jit(solution)/shard_map/pallas_call | solution.py:268
  344.8 21.3 %shard_map.122 = (bf16[2,64,16,128]{3,2,1,0:T(8,128)(2,1)}, bf16[2,128,16,128]{3,2,1,0:T(8,128)(2,1)}, bf16[2,192,16,128]{3,2,1,0:T(8,128)(2,1)}, bf16[2,256,16,...) custom-call(s32[4]{0:T(128)} %pad_add_fusion.s_ref, ...), custom_call_target="tpu_custom_call" | custom-call | flops 2791728640 | bytes 50000000 | tf_op jit(solution)/shard_map/pallas_call | solution.py:268
  368.2 21.2 %collective-permute-done.17.refs_4_ = bf16[32,64,256]{2,1,0:T(8,128)(2,1)} collective-permute-done((bf16[32,64,256]{2,1,0:T(8,128)(2,1)S(1)}, bf16[32,64,256]{2,1,0:T(8,128)(2,1)}, u32[]{:S(2)}, u32[]{:S(2)}) %collective-permute-start.17) | collective-permute-done | bytes 1048608 | tf_op jit(solution)/shard_map/ppermute | solution.py:298
  391.3 20.2 %collective-permute-done.18.refs_5_ = bf16[32,64,256]{2,1,0:T(8,128)(2,1)} collective-permute-done((bf16[32,64,256]{2,1,0:T(8,128)(2,1)S(1)}, bf16[32,64,256]{2,1,0:T(8,128)(2,1)}, u32[]{:S(2)}, u32[]{:S(2)}) %collective-permute-start.18) | collective-permute-done | bytes 1048608 | tf_op jit(solution)/shard_map/ppermute | solution.py:298
  415.1 15.0 %shard_map.124.refs_8_.refs_4_ = bf16[512,32,256]{2,1,0:T(8,128)(2,1)} custom-call(s32[4]{0:T(128)} %pad_add_fusion.s_ref, bf16[2,512,512]{2,1,0:T(8,128)(2,1)} %constant.166.clone.tab_ref, bf16[32,64,256]{2,1,0:T(8,128)(2,1)} %get-tuple-element.139.refs_0_, bf16[32,64,256]{2,1,0:T(8,128)(2,1)} %collective-permute-done.14.refs_1_, ...), custom_call_target="tpu_custom_call" | custom-call | flops 8589934592 | bytes 25165824 | tf_op jit(solution)/shard_map/pallas_call | solution.py:268
  467.1 21.1 %shard_map.129 = (bf16[2,64,16,128]{3,2,1,0:T(8,128)(2,1)}, bf16[2,128,16,128]{3,2,1,0:T(8,128)(2,1)}, bf16[2,192,16,128]{3,2,1,0:T(8,128)(2,1)}, bf16[2,256,16,...) custom-call(s32[4]{0:T(128)} %pad_add_fusion.s_ref, ...), custom_call_target="tpu_custom_call" | custom-call | flops 2791728640 | bytes 50000000 | tf_op jit(solution)/shard_map/pallas_call | solution.py:268
  497.5 24.1 %shard_map.131 = (bf16[2,256,16,128]{3,2,1,0:T(8,128)(2,1)}, bf16[2,256,16,128]{3,2,1,0:T(8,128)(2,1)}, bf16[2,192,16,128]{3,2,1,0:T(8,128)(2,1)}, bf16[2,192,16,128]{3,2,1,0:T(8,128)(2,1)}) custom-call(s32[4]{0:T(128)} %pad_add_fusion.s_ref, bf16[128,256,128]{2,1,0:T(8,128)(2,1)} %get-tuple-element.242.refs_11_.wre, ...), custom_call_target="tpu_custom_call" | custom-call | flops 4294967296 | bytes 40000000 | tf_op jit(solution)/shard_map/pallas_call | solution.py:268
  521.8 15.5 %shard_map.130 = (bf16[2,128,16,128]{3,2,1,0:T(8,128)(2,1)}, bf16[2,128,16,128]{3,2,1,0:T(8,128)(2,1)}, bf16[2,64,16,128]{3,2,1,0:T(8,128)(2,1)}, bf16[2,64,16,128]{3,2,1,0:T(8,128)(2,1)}) custom-call(s32[4]{0:T(128)} %pad_add_fusion.s_ref, bf16[128,256,128]{2,1,0:T(8,128)(2,1)} %get-tuple-element.242.refs_11_.wre, ...), custom_call_target="tpu_custom_call" | custom-call | flops 2147483648 | bytes 40000000 | tf_op jit(solution)/shard_map/pallas_call | solution.py:268
  538.2 24.3 %shard_map.136 = (bf16[2,256,16,128]{3,2,1,0:T(8,128)(2,1)}, bf16[2,256,16,128]{3,2,1,0:T(8,128)(2,1)}, bf16[2,192,16,128]{3,2,1,0:T(8,128)(2,1)}, bf16[2,192,16,128]{3,2,1,0:T(8,128)(2,1)}) custom-call(s32[4]{0:T(128)} %pad_add_fusion.s_ref, bf16[128,256,128]{2,1,0:T(8,128)(2,1)} %get-tuple-element.240.refs_9_.wre, ...), custom_call_target="tpu_custom_call" | custom-call | flops 4294967296 | bytes 40000000 | tf_op jit(solution)/shard_map/pallas_call | solution.py:268
  563.8 15.5 %shard_map.135 = (bf16[2,128,16,128]{3,2,1,0:T(8,128)(2,1)}, bf16[2,128,16,128]{3,2,1,0:T(8,128)(2,1)}, bf16[2,64,16,128]{3,2,1,0:T(8,128)(2,1)}, bf16[2,64,16,128]{3,2,1,0:T(8,128)(2,1)}) custom-call(s32[4]{0:T(128)} %pad_add_fusion.s_ref, bf16[128,256,128]{2,1,0:T(8,128)(2,1)} %get-tuple-element.240.refs_9_.wre, ...), custom_call_target="tpu_custom_call" | custom-call | flops 2147483648 | bytes 40000000 | tf_op jit(solution)/shard_map/pallas_call | solution.py:268
  581.3 20.8 %shard_map.132 = (bf16[512,32,256]{2,1,0:T(8,128)(2,1)}, bf16[512,16,256]{2,1,0:T(8,128)(2,1)}, bf16[512,16,256]{2,1,0:T(8,128)(2,1)}) custom-call(s32[4]{0:T(128)} %pad_add_fusion.s_ref, bf16[64,2,32,256]{3,2,1,0:T(8,128)(2,1)} %constant.162.clone.refs_0_, bf16[128,2,32,256]{3,2,1,0:T(8,128)(2,1)} %constant.163.clone.refs_1_, ...), custom_call_target="tpu_custom_call" | custom-call | flops 2791728640 | bytes 50000000 | tf_op jit(solution)/shard_map/pallas_call | solution.py:268
  615.6 20.8 %shard_map.137 = (bf16[512,16,256]{2,1,0:T(8,128)(2,1)}, bf16[512,48,256]{2,1,0:T(8,128)(2,1)}) custom-call(s32[4]{0:T(128)} %pad_add_fusion.s_ref, bf16[64,2,32,256]{3,2,1,0:T(8,128)(2,1)} %constant.162.clone.refs_0_, bf16[128,2,32,256]{3,2,1,0:T(8,128)(2,1)} %constant.163.clone.refs_1_, bf16[192,2,32,256]{3,2,1,0:T(8,128)(2,1)} %constant.164.clone.refs_2_, ...), custom_call_target="tpu_custom_call" | custom-call | flops 2791728640 | bytes 50000000 | tf_op jit(solution)/shard_map/pallas_call | solution.py:268
  652.1 14.7 %shard_map.134 = (bf16[32,64,256]{2,1,0:T(8,128)(2,1)}, bf16[32,64,256]{2,1,0:T(8,128)(2,1)}, bf16[32,64,256]{2,1,0:T(8,128)(2,1)}, bf16[32,64,256]{2,1,0:T(8,12...) custom-call(s32[4]{0:T(128)} %pad_add_fusion.s_ref, ...), custom_call_target="tpu_custom_call" | custom-call | flops 8589934592 | bytes 25165824 | tf_op jit(solution)/shard_map/pallas_call | solution.py:268
  687.3 19.5 %shard_map.138 = (bf16[48,64,256]{2,1,0:T(8,128)(2,1)}, bf16[48,64,256]{2,1,0:T(8,128)(2,1)}, bf16[48,64,256]{2,1,0:T(8,128)(2,1)}, bf16[48,64,256]{2,1,0:T(8,12...) custom-call(s32[4]{0:T(128)} %pad_add_fusion.s_ref, ...), custom_call_target="tpu_custom_call" | custom-call | flops 12884901888 | bytes 37748736 | tf_op jit(solution)/shard_map/pallas_call | solution.py:268
  706.8 32.3 %collective-permute-done.78.refs_7_ = bf16[16,64,256]{2,1,0:T(8,128)(2,1)S(1)} collective-permute-done((bf16[16,64,256]{2,1,0:T(8,128)(2,1)S(1)}, bf16[16,64,256]{2,1,0:T(8,128)(2,1)S(1)}, u32[]{:S(2)}, u32[]{:S(2)}) %collective-permute-start.78) | collective-permute-done | bytes 524320 | tf_op jit(solution)/shard_map/ppermute | solution.py:298
  744.2 22.5 %collective-permute-done.58.refs_5_ = bf16[32,64,256]{2,1,0:T(8,128)(2,1)S(1)} collective-permute-done((bf16[32,64,256]{2,1,0:T(8,128)(2,1)}, bf16[32,64,256]{2,1,0:T(8,128)(2,1)S(1)}, u32[]{:S(2)}, u32[]{:S(2)}) %collective-permute-start.58) | collective-permute-done | bytes 1048608 | tf_op jit(solution)/shard_map/ppermute | solution.py:298
  767.2 32.8 %collective-permute-done.59.refs_6_ = bf16[32,64,256]{2,1,0:T(8,128)(2,1)S(1)} collective-permute-done((bf16[32,64,256]{2,1,0:T(8,128)(2,1)}, bf16[32,64,256]{2,1,0:T(8,128)(2,1)S(1)}, u32[]{:S(2)}, u32[]{:S(2)}) %collective-permute-start.59) | collective-permute-done | bytes 1048608 | tf_op jit(solution)/shard_map/ppermute | solution.py:298
  801.3 19.9 %collective-permute-done.60.refs_7_ = bf16[32,64,256]{2,1,0:T(8,128)(2,1)S(1)} collective-permute-done((bf16[32,64,256]{2,1,0:T(8,128)(2,1)}, bf16[32,64,256]{2,1,0:T(8,128)(2,1)S(1)}, u32[]{:S(2)}, u32[]{:S(2)}) %collective-permute-start.60) | collective-permute-done | bytes 1048608 | tf_op jit(solution)/shard_map/ppermute | solution.py:298
  824.7 30.2 %collective-permute-done.67.refs_3_ = bf16[48,64,256]{2,1,0:T(8,128)(2,1)} collective-permute-done((bf16[48,64,256]{2,1,0:T(8,128)(2,1)}, bf16[48,64,256]{2,1,0:T(8,128)(2,1)}, u32[]{:S(2)}, u32[]{:S(2)}) %collective-permute-start.67) | collective-permute-done | bytes 1572896 | tf_op jit(solution)/shard_map/ppermute | solution.py:298
  857.7 98.7 %collective-permute-done.69.refs_5_ = bf16[48,64,256]{2,1,0:T(8,128)(2,1)} collective-permute-done((bf16[48,64,256]{2,1,0:T(8,128)(2,1)}, bf16[48,64,256]{2,1,0:T(8,128)(2,1)}, u32[]{:S(2)}, u32[]{:S(2)}) %collective-permute-start.69) | collective-permute-done | bytes 1572896 | tf_op jit(solution)/shard_map/ppermute | solution.py:298
  970.4 15.1 %shard_map.140.refs_8_ = f32[4,2,2,64,64,256]{5,4,3,2,1,0:T(8,128)} custom-call(s32[4]{0:T(128)} %pad_add_fusion.s_ref, f32[4,2,2,64,64,256]{5,4,3,2,1,0:T(8,128)} %bitcast.4.refs_0_.refs_1_.refs_2_.refs_3_.refs_4_.refs_5_.refs_6_.refs_7_.f_ref, bf16[16,64,256]{2,1,0:T(8,128)(2,1)} %get-tuple-element.222.refs_0_, ...), custom_call_target="tpu_custom_call" | custom-call | flops 83886080 | bytes 20971520 | tf_op jit(solution)/shard_map/pallas_call | solution.py:268
  985.5 40.8 %shard_map.141.refs_8_ = f32[4,2,2,64,64,256]{5,4,3,2,1,0:T(8,128)} custom-call(s32[4]{0:T(128)} %pad_add_fusion.s_ref, f32[4,2,2,64,64,256]{5,4,3,2,1,0:T(8,128)} %bitcast.4.refs_0_.refs_1_.refs_2_.refs_3_.refs_4_.refs_5_.refs_6_.refs_7_.f_ref, bf16[48,64,256]{2,1,0:T(8,128)(2,1)} %get-tuple-element.213.refs_0_, ...), custom_call_target="tpu_custom_call", output_to_operand_aliasing={{}: (10, {})} | custom-call | flops 251658240 | bytes 62914560 | tf_op jit(solution)/shard_map/pallas_call | solution.py:268
  1026.3 28.1 %shard_map.142.refs_8_ = f32[4,2,2,64,64,256]{5,4,3,2,1,0:T(8,128)} custom-call(s32[4]{0:T(128)} %pad_add_fusion.s_ref, f32[4,2,2,64,64,256]{5,4,3,2,1,0:T(8,128)} %bitcast.4.refs_0_.refs_1_.refs_2_.refs_3_.refs_4_.refs_5_.refs_6_.refs_7_.f_ref, bf16[32,64,256]{2,1,0:T(8,128)(2,1)} %get-tuple-element.196.refs_0_, ...), custom_call_target="tpu_custom_call", output_to_operand_aliasing={{}: (10, {})} | custom-call | flops 167772160 | bytes 41943040 | tf_op jit(solution)/shard_map/pallas_call | solution.py:268
  1058.0 15.2 %shard_map.143 = f32[4,2,2,64,64,256]{5,4,3,2,1,0:T(8,128)} custom-call(s32[4]{0:T(128)} %pad_add_fusion.s_ref, f32[4,2,2,64,64,256]{5,4,3,2,1,0:T(8,128)} %bitcast.4.refs_0_.refs_1_.refs_2_.refs_3_.refs_4_.refs_5_.refs_6_.refs_7_.f_ref, bf16[16,64,256]{2,1,0:T(8,128)(2,1)} %get-tuple-element.187.refs_0_, ...), custom_call_target="tpu_custom_call", output_to_operand_aliasing={{}: (10, {})} | custom-call | flops 83886080 | bytes 20971520 | tf_op jit(solution)/shard_map/pallas_call | solution.py:268
  1087.9 16.0 %collective-permute-done.83 = bf16[16,64,256]{2,1,0:T(8,128)(2,1)S(1)} collective-permute-done((bf16[16,64,256]{2,1,0:T(8,128)(2,1)S(1)}, bf16[16,64,256]{2,1,0:T(8,128)(2,1)S(1)}, u32[]{:S(2)}, u32[]{:S(2)}) %collective-permute-start.83) | collective-permute-done | bytes 524320 | tf_op jit(solution)/shard_map/ppermute | solution.py:298
  (271 shorter events, 276.7 us)
Async XLA Ops:
  103.2 82.3 %collective-permute-start.7 = (bf16[48,64,256]{2,1,0:T(8,128)(2,1)}, bf16[48,64,256]{2,1,0:T(8,128)(2,1)S(1)}, u32[]{:S(2)}, u32[]{:S(2)}) collective-permute-start(bf16[48,64,256]{2,1,0:T(8,128)(2,1)} %get-tuple-element.131), channel_id=1, source_target_pairs={{0,1},{1,0},{2,3},{3,2},{4,5},{5,4},{6,7},{7,6}} | collective-permute-start | bytes 4718600 | tf_op jit(solution)/shard_map/ppermute | solution.py:298
  112.2 75.4 %collective-permute-start.8 = (bf16[48,64,256]{2,1,0:T(8,128)(2,1)}, bf16[48,64,256]{2,1,0:T(8,128)(2,1)S(1)}, u32[]{:S(2)}, u32[]{:S(2)}) collective-permute-start(bf16[48,64,256]{2,1,0:T(8,128)(2,1)} %get-tuple-element.132), channel_id=1, source_target_pairs={{0,2},{1,3},{2,0},{3,1},{4,6},{5,7},{6,4},{7,5}} | collective-permute-start | bytes 4718600 | tf_op jit(solution)/shard_map/ppermute | solution.py:298
  113.0 70.4 %collective-permute-start.14 = (bf16[32,64,256]{2,1,0:T(8,128)(2,1)}, bf16[32,64,256]{2,1,0:T(8,128)(2,1)}, u32[]{:S(2)}, u32[]{:S(2)}) collective-permute-start(bf16[32,64,256]{2,1,0:T(8,128)(2,1)} %get-tuple-element.140), channel_id=1, source_target_pairs={{0,1},{1,0},{2,3},{3,2},{4,5},{5,4},{6,7},{7,6}} | collective-permute-start | bytes 3145736 | tf_op jit(solution)/shard_map/ppermute | solution.py:298
  113.4 71.8 %collective-permute-start.15 = (bf16[32,64,256]{2,1,0:T(8,128)(2,1)}, bf16[32,64,256]{2,1,0:T(8,128)(2,1)}, u32[]{:S(2)}, u32[]{:S(2)}) collective-permute-start(bf16[32,64,256]{2,1,0:T(8,128)(2,1)} %get-tuple-element.141), channel_id=1, source_target_pairs={{0,2},{1,3},{2,0},{3,1},{4,6},{5,7},{6,4},{7,5}} | collective-permute-start | bytes 3145736 | tf_op jit(solution)/shard_map/ppermute | solution.py:298
  114.5 68.6 %collective-permute-start.29 = (bf16[16,64,256]{2,1,0:T(8,128)(2,1)}, bf16[16,64,256]{2,1,0:T(8,128)(2,1)}, u32[]{:S(2)}, u32[]{:S(2)}) collective-permute-start(bf16[16,64,256]{2,1,0:T(8,128)(2,1)} %get-tuple-element.158), channel_id=1, source_target_pairs={{0,2},{1,3},{2,0},{3,1},{4,6},{5,7},{6,4},{7,5}} | collective-permute-start | bytes 1572872 | tf_op jit(solution)/shard_map/ppermute | solution.py:298
  183.4 104.3 %collective-permute-start.10 = (bf16[48,64,256]{2,1,0:T(8,128)(2,1)}, bf16[48,64,256]{2,1,0:T(8,128)(2,1)}, u32[]{:S(2)}, u32[]{:S(2)}) collective-permute-start(bf16[48,64,256]{2,1,0:T(8,128)(2,1)} %get-tuple-element.134), channel_id=1, source_target_pairs={{0,4},{1,5},{2,6},{3,7},{4,0},{5,1},{6,2},{7,3}} | collective-permute-start | bytes 4718600 | tf_op jit(solution)/shard_map/ppermute | solution.py:298
  185.2 136.4 %collective-permute-start.11 = (bf16[48,64,256]{2,1,0:T(8,128)(2,1)}, bf16[48,64,256]{2,1,0:T(8,128)(2,1)}, u32[]{:S(2)}, u32[]{:S(2)}) collective-permute-start(bf16[48,64,256]{2,1,0:T(8,128)(2,1)} %get-tuple-element.135), channel_id=1, source_target_pairs={{0,5},{1,4},{2,7},{3,6},{4,1},{5,0},{6,3},{7,2}} | collective-permute-start | bytes 4718600 | tf_op jit(solution)/shard_map/ppermute | solution.py:298
  185.4 137.9 %collective-permute-start.12 = (bf16[48,64,256]{2,1,0:T(8,128)(2,1)}, bf16[48,64,256]{2,1,0:T(8,128)(2,1)}, u32[]{:S(2)}, u32[]{:S(2)}) collective-permute-start(bf16[48,64,256]{2,1,0:T(8,128)(2,1)} %get-tuple-element.136), channel_id=1, source_target_pairs={{0,6},{1,7},{2,4},{3,5},{4,2},{5,3},{6,0},{7,1}} | collective-permute-start | bytes 4718600 | tf_op jit(solution)/shard_map/ppermute | solution.py:298
  187.6 136.4 %collective-permute-start.13 = (bf16[48,64,256]{2,1,0:T(8,128)(2,1)}, bf16[48,64,256]{2,1,0:T(8,128)(2,1)}, u32[]{:S(2)}, u32[]{:S(2)}) collective-permute-start(bf16[48,64,256]{2,1,0:T(8,128)(2,1)} %get-tuple-element.137), channel_id=1, source_target_pairs={{0,7},{1,6},{2,5},{3,4},{4,3},{5,2},{6,1},{7,0}} | collective-permute-start | bytes 4718600 | tf_op jit(solution)/shard_map/ppermute | solution.py:298
  221.5 144.7 %collective-permute-start.16 = (bf16[32,64,256]{2,1,0:T(8,128)(2,1)}, bf16[32,64,256]{2,1,0:T(8,128)(2,1)}, u32[]{:S(2)}, u32[]{:S(2)}) collective-permute-start(bf16[32,64,256]{2,1,0:T(8,128)(2,1)} %get-tuple-element.142), channel_id=1, source_target_pairs={{0,3},{1,2},{2,1},{3,0},{4,7},{5,6},{6,5},{7,4}} | collective-permute-start | bytes 3145736 | tf_op jit(solution)/shard_map/ppermute | solution.py:298
  287.7 101.8 %collective-permute-start.17 = (bf16[32,64,256]{2,1,0:T(8,128)(2,1)S(1)}, bf16[32,64,256]{2,1,0:T(8,128)(2,1)}, u32[]{:S(2)}, u32[]{:S(2)}) collective-permute-start(bf16[32,64,256]{2,1,0:T(8,128)(2,1)S(1)} %copy-done.32), channel_id=1, source_target_pairs={{0,4},{1,5},{2,6},{3,7},{4,0},{5,1},{6,2},{7,3}} | collective-permute-start | bytes 3145736 | tf_op jit(solution)/shard_map/ppermute | solution.py:298
  321.6 89.9 %collective-permute-start.18 = (bf16[32,64,256]{2,1,0:T(8,128)(2,1)S(1)}, bf16[32,64,256]{2,1,0:T(8,128)(2,1)}, u32[]{:S(2)}, u32[]{:S(2)}) collective-permute-start(bf16[32,64,256]{2,1,0:T(8,128)(2,1)S(1)} %copy-done.31), channel_id=1, source_target_pairs={{0,5},{1,4},{2,7},{3,6},{4,1},{5,0},{6,3},{7,2}} | collective-permute-start | bytes 3145736 | tf_op jit(solution)/shard_map/ppermute | solution.py:298
  323.3 89.9 %collective-permute-start.19 = (bf16[32,64,256]{2,1,0:T(8,128)(2,1)S(1)}, bf16[32,64,256]{2,1,0:T(8,128)(2,1)}, u32[]{:S(2)}, u32[]{:S(2)}) collective-permute-start(bf16[32,64,256]{2,1,0:T(8,128)(2,1)S(1)} %copy-done.30), channel_id=1, source_target_pairs={{0,6},{1,7},{2,4},{3,5},{4,2},{5,3},{6,0},{7,1}} | collective-permute-start | bytes 3145736 | tf_op jit(solution)/shard_map/ppermute | solution.py:298
  324.0 89.9 %collective-permute-start.20 = (bf16[32,64,256]{2,1,0:T(8,128)(2,1)S(1)}, bf16[32,64,256]{2,1,0:T(8,128)(2,1)}, u32[]{:S(2)}, u32[]{:S(2)}) collective-permute-start(bf16[32,64,256]{2,1,0:T(8,128)(2,1)S(1)} %copy-done.29), channel_id=1, source_target_pairs={{0,7},{1,6},{2,5},{3,4},{4,3},{5,2},{6,1},{7,0}} | collective-permute-start | bytes 3145736 | tf_op jit(solution)/shard_map/ppermute | solution.py:298
  366.1 73.6 %collective-permute-start.30 = (bf16[16,64,256]{2,1,0:T(8,128)(2,1)S(1)}, bf16[16,64,256]{2,1,0:T(8,128)(2,1)S(1)}, u32[]{:S(2)}, u32[]{:S(2)}) collective-permute-start(bf16[16,64,256]{2,1,0:T(8,128)(2,1)S(1)} %copy-done.39), channel_id=1, source_target_pairs={{0,3},{1,2},{2,1},{3,0},{4,7},{5,6},{6,5},{7,4}} | collective-permute-start | bytes 1572872 | tf_op jit(solution)/shard_map/ppermute | solution.py:298
  521.6 58.3 %collective-permute-start.46 = (bf16[2,256,16,128]{3,2,1,0:T(8,128)(2,1)}, bf16[2,256,16,128]{3,2,1,0:T(8,128)(2,1)S(1)}, u32[]{:S(2)}, u32[]{:S(2)}) collective-permute-start(bf16[2,256,16,128]{3,2,1,0:T(8,128)(2,1)} %get-tuple-element.185), channel_id=1, source_target_pairs={{0,1},{1,0},{2,3},{3,2},{4,5},{5,4},{6,7},{7,6}} | collective-permute-start | bytes 6291464 | tf_op jit(solution)/shard_map/ppermute | solution.py:298
  667.6 72.3 %collective-permute-start.54 = (bf16[32,64,256]{2,1,0:T(8,128)(2,1)}, bf16[32,64,256]{2,1,0:T(8,128)(2,1)S(1)}, u32[]{:S(2)}, u32[]{:S(2)}) collective-permute-start(bf16[32,64,256]{2,1,0:T(8,128)(2,1)} %get-tuple-element.197), channel_id=1, source_target_pairs={{0,1},{1,0},{2,3},{3,2},{4,5},{5,4},{6,7},{7,6}} | collective-permute-start | bytes 3145736 | tf_op jit(solution)/shard_map/ppermute | solution.py:298
  672.4 68.7 %collective-permute-start.55 = (bf16[32,64,256]{2,1,0:T(8,128)(2,1)}, bf16[32,64,256]{2,1,0:T(8,128)(2,1)S(1)}, u32[]{:S(2)}, u32[]{:S(2)}) collective-permute-start(bf16[32,64,256]{2,1,0:T(8,128)(2,1)} %get-tuple-element.198), channel_id=1, source_target_pairs={{0,2},{1,3},{2,0},{3,1},{4,6},{5,7},{6,4},{7,5}} | collective-permute-start | bytes 3145736 | tf_op jit(solution)/shard_map/ppermute | solution.py:298
  673.1 68.1 %collective-permute-start.56 = (bf16[32,64,256]{2,1,0:T(8,128)(2,1)}, bf16[32,64,256]{2,1,0:T(8,128)(2,1)}, u32[]{:S(2)}, u32[]{:S(2)}) collective-permute-start(bf16[32,64,256]{2,1,0:T(8,128)(2,1)} %get-tuple-element.199), channel_id=1, source_target_pairs={{0,3},{1,2},{2,1},{3,0},{4,7},{5,6},{6,5},{7,4}} | collective-permute-start | bytes 3145736 | tf_op jit(solution)/shard_map/ppermute | solution.py:298
  739.1 84.2 %collective-permute-start.65 = (bf16[48,64,256]{2,1,0:T(8,128)(2,1)}, bf16[48,64,256]{2,1,0:T(8,128)(2,1)S(1)}, u32[]{:S(2)}, u32[]{:S(2)}) collective-permute-start(bf16[48,64,256]{2,1,0:T(8,128)(2,1)} %get-tuple-element.214), channel_id=1, source_target_pairs={{0,1},{1,0},{2,3},{3,2},{4,5},{5,4},{6,7},{7,6}} | collective-permute-start | bytes 4718600 | tf_op jit(solution)/shard_map/ppermute | solution.py:298
  739.9 84.7 %collective-permute-start.66 = (bf16[48,64,256]{2,1,0:T(8,128)(2,1)}, bf16[48,64,256]{2,1,0:T(8,128)(2,1)S(1)}, u32[]{:S(2)}, u32[]{:S(2)}) collective-permute-start(bf16[48,64,256]{2,1,0:T(8,128)(2,1)} %get-tuple-element.215), channel_id=1, source_target_pairs={{0,2},{1,3},{2,0},{3,1},{4,6},{5,7},{6,4},{7,5}} | collective-permute-start | bytes 4718600 | tf_op jit(solution)/shard_map/ppermute | solution.py:298
  741.2 58.8 %collective-permute-start.59 = (bf16[32,64,256]{2,1,0:T(8,128)(2,1)}, bf16[32,64,256]{2,1,0:T(8,128)(2,1)S(1)}, u32[]{:S(2)}, u32[]{:S(2)}) collective-permute-start(bf16[32,64,256]{2,1,0:T(8,128)(2,1)} %get-tuple-element.202), channel_id=1, source_target_pairs={{0,6},{1,7},{2,4},{3,5},{4,2},{5,3},{6,0},{7,1}} | collective-permute-start | bytes 3145736 | tf_op jit(solution)/shard_map/ppermute | solution.py:298
  742.8 78.4 %collective-permute-start.60 = (bf16[32,64,256]{2,1,0:T(8,128)(2,1)}, bf16[32,64,256]{2,1,0:T(8,128)(2,1)S(1)}, u32[]{:S(2)}, u32[]{:S(2)}) collective-permute-start(bf16[32,64,256]{2,1,0:T(8,128)(2,1)} %get-tuple-element.203), channel_id=1, source_target_pairs={{0,7},{1,6},{2,5},{3,4},{4,3},{5,2},{6,1},{7,0}} | collective-permute-start | bytes 3145736 | tf_op jit(solution)/shard_map/ppermute | solution.py:298
  766.7 88.2 %collective-permute-start.67 = (bf16[48,64,256]{2,1,0:T(8,128)(2,1)}, bf16[48,64,256]{2,1,0:T(8,128)(2,1)}, u32[]{:S(2)}, u32[]{:S(2)}) collective-permute-start(bf16[48,64,256]{2,1,0:T(8,128)(2,1)} %get-tuple-element.216), channel_id=1, source_target_pairs={{0,3},{1,2},{2,1},{3,0},{4,7},{5,6},{6,5},{7,4}} | collective-permute-start | bytes 4718600 | tf_op jit(solution)/shard_map/ppermute | solution.py:298
  821.2 135.1 %collective-permute-start.69 = (bf16[48,64,256]{2,1,0:T(8,128)(2,1)}, bf16[48,64,256]{2,1,0:T(8,128)(2,1)}, u32[]{:S(2)}, u32[]{:S(2)}) collective-permute-start(bf16[48,64,256]{2,1,0:T(8,128)(2,1)} %get-tuple-element.218), channel_id=1, source_target_pairs={{0,5},{1,4},{2,7},{3,6},{4,1},{5,0},{6,3},{7,2}} | collective-permute-start | bytes 4718600 | tf_op jit(solution)/shard_map/ppermute | solution.py:298
  823.3 135.1 %collective-permute-start.70 = (bf16[48,64,256]{2,1,0:T(8,128)(2,1)}, bf16[48,64,256]{2,1,0:T(8,128)(2,1)}, u32[]{:S(2)}, u32[]{:S(2)}) collective-permute-start(bf16[48,64,256]{2,1,0:T(8,128)(2,1)} %get-tuple-element.219), channel_id=1, source_target_pairs={{0,6},{1,7},{2,4},{3,5},{4,2},{5,3},{6,0},{7,1}} | collective-permute-start | bytes 4718600 | tf_op jit(solution)/shard_map/ppermute | solution.py:298
  824.7 143.9 %collective-permute-start.71 = (bf16[48,64,256]{2,1,0:T(8,128)(2,1)}, bf16[48,64,256]{2,1,0:T(8,128)(2,1)S(1)}, u32[]{:S(2)}, u32[]{:S(2)}) collective-permute-start(bf16[48,64,256]{2,1,0:T(8,128)(2,1)} %get-tuple-element.220), channel_id=1, source_target_pairs={{0,7},{1,6},{2,5},{3,4},{4,3},{5,2},{6,1},{7,0}} | collective-permute-start | bytes 4718600 | tf_op jit(solution)/shard_map/ppermute | solution.py:298
  854.9 199.5 %collective-permute-start.50 = (bf16[16,64,256]{2,1,0:T(8,128)(2,1)}, bf16[16,64,256]{2,1,0:T(8,128)(2,1)}, u32[]{:S(2)}, u32[]{:S(2)}) collective-permute-start(bf16[16,64,256]{2,1,0:T(8,128)(2,1)} %get-tuple-element.191), channel_id=1, source_target_pairs={{0,4},{1,5},{2,6},{3,7},{4,0},{5,1},{6,2},{7,3}} | collective-permute-start | bytes 1572872 | tf_op jit(solution)/shard_map/ppermute | solution.py:298
  856.4 199.3 %collective-permute-start.51 = (bf16[16,64,256]{2,1,0:T(8,128)(2,1)}, bf16[16,64,256]{2,1,0:T(8,128)(2,1)}, u32[]{:S(2)}, u32[]{:S(2)}) collective-permute-start(bf16[16,64,256]{2,1,0:T(8,128)(2,1)} %get-tuple-element.192), channel_id=1, source_target_pairs={{0,5},{1,4},{2,7},{3,6},{4,1},{5,0},{6,3},{7,2}} | collective-permute-start | bytes 1572872 | tf_op jit(solution)/shard_map/ppermute | solution.py:298
  956.4 99.5 %collective-permute-start.52 = (bf16[16,64,256]{2,1,0:T(8,128)(2,1)}, bf16[16,64,256]{2,1,0:T(8,128)(2,1)}, u32[]{:S(2)}, u32[]{:S(2)}) collective-permute-start(bf16[16,64,256]{2,1,0:T(8,128)(2,1)} %get-tuple-element.193), channel_id=1, source_target_pairs={{0,6},{1,7},{2,4},{3,5},{4,2},{5,3},{6,0},{7,1}} | collective-permute-start | bytes 1572872 | tf_op jit(solution)/shard_map/ppermute | solution.py:298
  958.3 98.8 %collective-permute-start.53 = (bf16[16,64,256]{2,1,0:T(8,128)(2,1)}, bf16[16,64,256]{2,1,0:T(8,128)(2,1)}, u32[]{:S(2)}, u32[]{:S(2)}) collective-permute-start(bf16[16,64,256]{2,1,0:T(8,128)(2,1)} %get-tuple-element.194), channel_id=1, source_target_pairs={{0,7},{1,6},{2,5},{3,4},{4,3},{5,2},{6,1},{7,0}} | collective-permute-start | bytes 1572872 | tf_op jit(solution)/shard_map/ppermute | solution.py:298
  969.7 106.0 %collective-permute-start.79 = (bf16[16,64,256]{2,1,0:T(8,128)(2,1)}, bf16[16,64,256]{2,1,0:T(8,128)(2,1)}, u32[]{:S(2)}, u32[]{:S(2)}) collective-permute-start(bf16[16,64,256]{2,1,0:T(8,128)(2,1)} %get-tuple-element.232), channel_id=1, source_target_pairs={{0,1},{1,0},{2,3},{3,2},{4,5},{5,4},{6,7},{7,6}} | collective-permute-start | bytes 1572872 | tf_op jit(solution)/shard_map/ppermute | solution.py:298
  (100 other events, 3615.0 us)
